TPU v7x, 128 devices: a whole 4x4x4 slice. The times are simulated.
128 devices in a mesh: grp: 16 (over z, x), ep: 8 (over y, core).
Axes of the slice: x: 4, y: 4, z: 4, core: 2. Of those that a mesh axis runs over, the one named last changes fastest.
Arguments:
- tokens: bfloat16 [256, 7168], P(('grp', 'ep')), may hold values from -6 to 6
- expert_ids: int32 [256, 8], P(('grp', 'ep')), may hold values from 0 to 15, all different within a row; in each aligned block of 2 rows (0 to 1, 2 to 3, ...) at most 2 rows name the same one
- gate_ints: int32 [256, 8], P(('grp', 'ep')), may hold values from 1 to 16
- w_gate: bfloat16 [16, 7168, 2048], P('grp', None, 'ep'), may hold values from -0.0625 to 0.0625
- w_up: bfloat16 [16, 7168, 2048], P('grp', None, 'ep'), may hold values from -0.0625 to 0.0625
- w_down: bfloat16 [16, 2048, 7168], P('grp', 'ep'), may hold values from -0.125 to 0.125
Outputs:
- mixed: bfloat16 [256, 7168], P(('grp', 'ep'))
Inputs may be any that keep to these rules, and one draw needn't show every extreme that they name: `expert_ids`: each row names 8 different experts. Within the 2 rows of one device no expert is named more than 2 times, a bound that some block reaches on some device in every draw.
All inputs are finite; a program needn't handle non-finite values.
Results may differ from a plain program's by a relative error of at most 0.015.
Values may be sent and summed in bfloat16 or wider, within the bound.
No kernel may reach another device: no remote copies, remote signals or barrier semaphores. Data moves between devices by JAX's collectives and lax.ppermute only.
A program may use at most 64 MiB of HBM per device.

v0:
```python
import itertools

import jax
import jax.numpy as jnp
from jax import lax
from jax.experimental import pallas as pl
from jax.experimental.pallas import tpu as pltpu
from jax.sharding import Mesh
from jax.sharding import PartitionSpec as P

ALL = ("z", "x", "y", "c")
RING = 4
LANES = 128
KCH = 1024
RATE = 250


def index(z, x, y, c):
    return ((z * RING + x) * RING + y) * 2 + c


def class_groups():
    groups = []
    for colour in range(RING):
        for c in range(2):
            members = []
            for z, y in itertools.product(range(RING), repeat=2):
                members.append(index(z, (colour + 2 * y + z) % RING, y, c))
            groups.append(members)
    return groups


def neighbour_pairs(axis, back):
    pairs = []
    for z, x, y in itertools.product(range(RING), repeat=3):
        for c in range(2):
            there = {"z": z, "x": x, "y": y}
            there[axis] = (there[axis] + (1 if c == 0 else -1)) % RING
            pair = (index(z, x, y, c), index(there["z"], there["x"], there["y"], c))
            pairs.append(pair[::-1] if back else pair)
    return pairs


def swap_pairs():
    return [(i, i ^ 1) for i in range(2 * RING**3)]


def head_kernel(me_ref, tok_hbm, ids_hbm, ints_hbm, out_ref, tok, ids_ref, ints_ref, sems):
    width = tok.shape[1]
    copies = [
        pltpu.make_async_copy(src, dst, sems.at[i])
        for i, (src, dst) in enumerate(((ids_hbm, ids_ref), (ints_hbm, ints_ref), (tok_hbm, tok)))
    ]
    for copy in copies:
        copy.start()
    for copy in copies:
        copy.wait()
    ids, ints = ids_ref[...], ints_ref[...]
    lane = lax.broadcasted_iota(jnp.int32, (ids.shape[0], LANES), 1)
    scores = jnp.zeros(lane.shape, jnp.float32)
    for k in range(ids.shape[1]):
        scores += jnp.where(ids[:, k:k + 1] == lane, ints[:, k:k + 1], 0).astype(jnp.float32)
    scores = scores.astype(jnp.bfloat16)
    token = tok[...]
    for i in range(out_ref.shape[0]):
        out_ref[i, :, :width] = token
        out_ref[i, :, width:] = scores


def load_kernel(wg_hbm, wu_hbm, wd_hbm, after_ref, wg, wu, wd, sems):
    copies = [
        pltpu.make_async_copy(src, dst, sems.at[i])
        for i, (src, dst) in enumerate(((wg_hbm, wg), (wu_hbm, wu), (wd_hbm, wd)))
    ]
    for copy in copies:
        copy.start()
    for copy in copies:
        copy.wait()


def experts_kernel(me_ref, mine_in, theirs_in, wg, wu, wd, after_ref, mine_out, theirs_out, hid):
    width = wg.shape[0]
    size = mine_in.shape[0]

    def rows(ks):
        return jnp.concatenate([mine_in[:, ks], theirs_in[:, ks]], axis=0)

    scores = rows(pl.ds(width, LANES)).astype(jnp.float32)
    lane = lax.broadcasted_iota(jnp.int32, scores.shape, 1)
    picked = jnp.sum(jnp.where(lane == me_ref[0], scores, 0.0), axis=1, keepdims=True)
    weight = picked / jnp.sum(scores, axis=1, keepdims=True)
    gate = up = None
    for i in range(width // KCH):
        ks = pl.ds(i * KCH, KCH)
        part = rows(ks)
        g = jnp.dot(part, wg[ks, :], preferred_element_type=jnp.float32)
        u = jnp.dot(part, wu[ks, :], preferred_element_type=jnp.float32)
        gate, up = (g, u) if gate is None else (gate + g, up + u)
    hid[...] = (gate / (1.0 + jnp.exp(-gate)) * up).astype(jnp.bfloat16)
    for i in range(width // KCH):
        ks = pl.ds(i * KCH, KCH)
        out = jnp.dot(hid[...], wd[:, ks], preferred_element_type=jnp.float32) * weight
        mine_out[:, ks] = out[:size]
        theirs_out[:, ks] = out[size:].astype(jnp.bfloat16)


def run_experts(me, mine, theirs, weights, after):
    size = mine.shape[0]
    width, hidden = weights[0].shape
    return pl.pallas_call(
        experts_kernel,
        out_shape=(
            jax.ShapeDtypeStruct((size, width), jnp.float32),
            jax.ShapeDtypeStruct((size, width), jnp.bfloat16),
        ),
        in_specs=[SMEM] + [VMEM] * 5 + [pl.BlockSpec(memory_space=pl.ANY)],
        out_specs=(VMEM, VMEM),
        scratch_shapes=[pltpu.VMEM((2 * size, hidden), jnp.bfloat16)],
        compiler_params=LIMIT,
        cost_estimate=cost(1.0),
    )(me, mine, theirs, *weights, after)


VMEM = pl.BlockSpec(memory_space=pltpu.VMEM)
SMEM = pl.BlockSpec(memory_space=pltpu.SMEM)
HBM = pl.BlockSpec(memory_space=pltpu.HBM)
LIMIT = pltpu.CompilerParams(vmem_limit_bytes=24 * 1024 * 1024)


def cost(us):
    return pl.CostEstimate(flops=int(us * 1e6 * RATE), transcendentals=0, bytes_accessed=0)


def in_hbm(*arrays):
    return [pltpu.with_memory_space_constraint(a, pltpu.HBM) for a in arrays]


def moved(block, pairs):
    return lax.ppermute(block, ALL, pairs)


def step(tokens, expert_ids, gate_ints, w_gate, w_up, w_down):
    width = tokens.shape[1]
    me = (lax.axis_index("z") * RING + lax.axis_index("x")).astype(jnp.int32).reshape(1)
    groups = class_groups()
    n = len(groups[0])
    bf16, f32 = jnp.bfloat16, jnp.float32

    tiled = pl.pallas_call(
        head_kernel,
        out_shape=jax.ShapeDtypeStruct((n, tokens.shape[0], width + LANES), bf16),
        in_specs=[SMEM] + [HBM] * 3,
        out_specs=VMEM,
        scratch_shapes=[
            pltpu.VMEM(tokens.shape, bf16),
            pltpu.VMEM(expert_ids.shape, jnp.int32),
            pltpu.VMEM(gate_ints.shape, jnp.int32),
            pltpu.SemaphoreType.DMA((3,)),
        ],
        compiler_params=LIMIT,
        name="head",
    )(me, *in_hbm(tokens, expert_ids, gate_ints))
    own = lax.all_to_all(tiled, ALL, split_axis=0, concat_axis=0, axis_index_groups=groups, tiled=True)
    own = own.reshape(n * tokens.shape[0], width + LANES)
    wg, wu, wd = pl.pallas_call(
        load_kernel,
        out_shape=[jax.ShapeDtypeStruct(w.shape[1:], bf16) for w in (w_gate, w_up, w_down)],
        in_specs=[HBM] * 3 + [pl.BlockSpec(memory_space=pl.ANY)],
        out_specs=[VMEM] * 3,
        scratch_shapes=[pltpu.SemaphoreType.DMA((3,))],
        compiler_params=LIMIT,
        cost_estimate=cost(3.4),
        name="load",
    )(*in_hbm(w_gate[0], w_up[0], w_down[0]), own)

    near = {a: moved(own, neighbour_pairs(a, False)) for a in "xyz"}
    near["o"] = own
    swapped = {a: moved(b, swap_pairs()) for a, b in near.items()}
    total = {}
    after = me
    for a in "oxyz":
        mine, theirs = run_experts(me, near[a], swapped[a], (wg, wu, wd), after)
        after = theirs
        total[a] = mine + moved(theirs, swap_pairs()).astype(f32)
    acc = total["o"]
    for a in "xyz":
        acc = acc + moved(total[a].astype(bf16), neighbour_pairs(a, True)).astype(f32)
    pieces = acc.astype(bf16).reshape(n, tokens.shape[0], width)
    got = lax.all_to_all(pieces, ALL, split_axis=0, concat_axis=0, axis_index_groups=groups, tiled=True)
    return jnp.sum(got.astype(f32), axis=0).astype(bf16)


def solution(mesh):
    fine = Mesh(mesh.devices.reshape(RING, RING, RING, 2), ALL)
    in_specs = (
        P(ALL, None),
        P(ALL, None),
        P(ALL, None),
        P(("z", "x"), None, ("y", "c")),
        P(("z", "x"), None, ("y", "c")),
        P(("z", "x"), ("y", "c"), None),
    )
    return jax.shard_map(step, mesh=fine, in_specs=in_specs, out_specs=P(ALL, None), check_vma=False)
```

profile of v0, /device:TPU:0, one launch (start us, length us, event | category | flops | bytes accessed | tf_op | source)
XLA Modules:
  0.0 79.0 jit_solution(6177516972368587031)
XLA Ops:
  0.0 0.9 %head.1 = bf16[16,2,7296]{2,1,0:T(2,128)(2,1)S(1)} custom-call(s32[1]{0:T(128)} %bitcast.me_ref.after_ref, bf16[2,7168]{1,0:T(2,128)(2,1)} %tok_hbm.1, s32[2,8]{1,0:T(2,128)} %ids_hbm.1, s32[2,8]{1,0:T(2,128)} %ints_hbm.1), custom_call_target="tpu_custom_call" | custom-call | tf_op jit(solution)/shard_map/head/pallas_call | solution.py:149
  0.9 22.9 %all_to_all.10 = bf16[16,2,7296]{2,1,0:T(2,128)(2,1)S(1)} all-to-all(bf16[16,2,7296]{2,1,0:T(2,128)(2,1)S(1)} %head.1), channel_id=1, replica_groups={{0,18,4,22,40,58,44,62,80,66,84,70,120,106,124,110},{1,19,5,23,41,59,45..., dimensions={0} | all-to-all | bytes 933888 | tf_op jit(solution)/shard_map/all_to_all | solution.py:163
  23.8 0.2 reshape.10.after_ref.mine_in
  24.0 0.1 collective-permute-start.2
  24.1 0.8 %collective-permute-start.6 = (bf16[32,7296]{1,0:T(8,128)(2,1)S(1)}, bf16[32,7296]{1,0:T(8,128)(2,1)S(1)}, u32[]{:S(2)}, u32[]{:S(2)}) collective-permute-start(bf16[32,7296]{1,0:T(8,128)(2,1)S(1)} %reshape.10.after_ref.mine_in), channel_id=1, source_target_pairs={{0,2},{1,7},{2,4},{3,1},{4,6},{5,3},{6,0},{7,5},{8,10},{9,15},{10,... | collective-permute-start | bytes 1400840 | tf_op jit(solution)/shard_map/ppermute | solution.py:139
  24.9 8.9 %collective-permute-done.2.mine_in = bf16[32,7296]{1,0:T(8,128)(2,1)S(1)} collective-permute-done((bf16[32,7296]{1,0:T(8,128)(2,1)S(1)}, bf16[32,7296]{1,0:T(8,128)(2,1)S(1)}, u32[]{:S(2)}, u32[]{:S(2)}) %collective-permute-start.2) | collective-permute-done | bytes 466976 | tf_op jit(solution)/shard_map/ppermute | solution.py:139
  33.9 0.0 collective-permute-start.3
  33.9 0.1 collective-permute-done.6.mine_in
  33.9 0.4 collective-permute-start.7
  34.4 4.2 %load.1 = (bf16[7168,256]{1,0:T(8,128)(2,1)S(1)}, bf16[7168,256]{1,0:T(8,128)(2,1)S(1)}, bf16[256,7168]{1,0:T(8,128)(2,1)S(1)}) custom-call(bf16[7168,256]{1,0:T(8,128)(2,1)} %bitcast.4, bf16[7168,256]{1,0:T(8,128)(2,1)} %bitcast.5, bf16[256,7168]{1,0:T(8,128)(2,1)} %bitcast.6, bf16[32,7296]{1,0:T(8,128)(2,1)S(1)} %reshape.10.after_ref.mine_in), custom_call_target="tpu_custom_call" | custom-call | flops 850000000 | tf_op jit(solution)/shard_map/load/pallas_call | solution.py:165
  38.6 0.2 collective-permute-start.11
  38.8 2.1 %shard_map.64 = (f32[32,7168]{1,0:T(8,128)S(1)}, bf16[32,7168]{1,0:T(8,128)(2,1)S(1)}) custom-call(s32[1]{0:T(128)} %bitcast.me_ref.after_ref, bf16[32,7296]{1,0:T(8,128)(2,1)S(1)} %reshape.10.after_ref.mine_in, bf16[32,7296]{1,0:T(8,128)(2,1)S(1)} %collective-permute-done.theirs_in, bf16[7168,256]{1,0:T(8,128)(2,1)S(1)} %get-tuple-element.16.wg, ...), custom_call_target="tpu_custom_call" | custom-call | flops 250000000 | tf_op jit(solution)/shard_map/pallas_call | solution.py:110
  40.9 2.1 %shard_map.65 = (f32[32,7168]{1,0:T(8,128)S(1)}, bf16[32,7168]{1,0:T(8,128)(2,1)S(1)}) custom-call(s32[1]{0:T(128)} %bitcast.me_ref.after_ref, bf16[32,7296]{1,0:T(8,128)(2,1)S(1)} %collective-permute-done.2.mine_in, bf16[32,7296]{1,0:T(8,128)(2,1)S(1)} %collective-permute-done.3.theirs_in, bf16[7168,256]{1,0:T(8,128)(2,1)S(1)} %get-tuple-element.16.wg, ...), custom_call_target="tpu_custom_call" | custom-call | flops 250000000 | tf_op jit(solution)/shard_map/pallas_call | solution.py:110
  43.1 0.5 collective-permute-start.4
  43.6 0.1 collective-permute-start.1
  43.7 2.1 %shard_map.66 = (f32[32,7168]{1,0:T(8,128)S(1)}, bf16[32,7168]{1,0:T(8,128)(2,1)S(1)}) custom-call(s32[1]{0:T(128)} %bitcast.me_ref.after_ref, bf16[32,7296]{1,0:T(8,128)(2,1)S(1)} %collective-permute-done.6.mine_in, bf16[32,7296]{1,0:T(8,128)(2,1)S(1)} %collective-permute-done.7.theirs_in, bf16[7168,256]{1,0:T(8,128)(2,1)S(1)} %get-tuple-element.16.wg, ...), custom_call_target="tpu_custom_call" | custom-call | flops 250000000 | tf_op jit(solution)/shard_map/pallas_call | solution.py:110
  45.8 0.5 collective-permute-start.8
  46.3 2.1 %shard_map.67 = (f32[32,7168]{1,0:T(8,128)S(1)}, bf16[32,7168]{1,0:T(8,128)(2,1)S(1)}) custom-call(s32[1]{0:T(128)} %bitcast.me_ref.after_ref, bf16[32,7296]{1,0:T(8,128)(2,1)S(1)} %collective-permute-done.10.mine_in, bf16[32,7296]{1,0:T(8,128)(2,1)S(1)} %collective-permute-done.11.theirs_in, bf16[7168,256]{1,0:T(8,128)(2,1)S(1)} %get-tuple-element.16.wg, ...), custom_call_target="tpu_custom_call" | custom-call | flops 250000000 | tf_op jit(solution)/shard_map/pallas_call | solution.py:110
  48.5 0.2 collective-permute-start.12
  48.6 0.1 add_convert_fusion.3
  48.7 3.2 %collective-permute-start.5 = (bf16[32,7168]{1,0:T(8,128)(2,1)S(1)}, bf16[32,7168]{1,0:T(8,128)(2,1)S(1)}, u32[]{:S(2)}, u32[]{:S(2)}) collective-permute-start(bf16[32,7168]{1,0:T(8,128)(2,1)S(1)} %add_convert_fusion.3), channel_id=1, source_target_pairs={{8,0},{25,1},{10,2},{27,3},{12,4},{29,5},{14,6},{31,7},{16,8},{1,9... | collective-permute-start | bytes 1376264 | tf_op jit(solution)/shard_map/ppermute | solution.py:139
  52.0 0.1 add_convert_fusion.2
  52.0 0.1 collective-permute-start.9
  52.1 0.1 add_convert_fusion.1
  52.2 1.3 %collective-permute-start.13 = (bf16[32,7168]{1,0:T(8,128)(2,1)S(1)}, bf16[32,7168]{1,0:T(8,128)(2,1)S(1)}, u32[]{:S(2)}, u32[]{:S(2)}) collective-permute-start(bf16[32,7168]{1,0:T(8,128)(2,1)S(1)} %add_convert_fusion.1), channel_id=1, source_target_pairs={{32,0},{97,1},{34,2},{99,3},{36,4},{101,5},{38,6},{103,7},{40,8},{... | collective-permute-start | bytes 1376264 | tf_op jit(solution)/shard_map/ppermute | solution.py:139
  53.5 4.4 %collective-permute-done.5 = bf16[32,7168]{1,0:T(8,128)(2,1)S(1)} collective-permute-done((bf16[32,7168]{1,0:T(8,128)(2,1)S(1)}, bf16[32,7168]{1,0:T(8,128)(2,1)S(1)}, u32[]{:S(2)}, u32[]{:S(2)}) %collective-permute-start.5) | collective-permute-done | bytes 458784 | tf_op jit(solution)/shard_map/ppermute | solution.py:139
  58.0 2.6 %collective-permute-done.9 = bf16[32,7168]{1,0:T(8,128)(2,1)S(1)} collective-permute-done((bf16[32,7168]{1,0:T(8,128)(2,1)S(1)}, bf16[32,7168]{1,0:T(8,128)(2,1)S(1)}, u32[]{:S(2)}, u32[]{:S(2)}) %collective-permute-start.9) | collective-permute-done | bytes 458784 | tf_op jit(solution)/shard_map/ppermute | solution.py:139
  60.6 0.2 collective-permute-done.13
  60.8 0.3 add_convert_fusion
  61.1 0.2 reshape.11
  61.3 16.7 %all_to_all.11 = bf16[16,2,7168]{2,1,0:T(2,128)(2,1)S(1)} all-to-all(bf16[16,2,7168]{2,1,0:T(2,128)(2,1)S(1)} %reshape.11), channel_id=1, replica_groups={{0,18,4,22,40,58,44,62,80,66,84,70,120,106,124,110},{1,19,5,23,41,59,45..., dimensions={0} | all-to-all | bytes 917504 | tf_op jit(solution)/shard_map/all_to_all | solution.py:189
  78.0 1.0 %reduce_sum.12 = bf16[2,7168]{1,0:T(2,128)(2,1)} reduce(bf16[16,2,7168]{2,1,0:T(2,128)(2,1)S(1)} %all_to_all.11, bf16[]{:T(256)} %constant.13.clone.1), dimensions={0}, to_apply=%region_0.0 | reduce | flops 215040 | bytes 487426 | tf_op jit(solution)/shard_map/reduce_sum | solution.py:190
  (11 shorter events, 0.0 us)
Async XLA Ops:
  24.0 9.8 %collective-permute-start.2 = (bf16[32,7296]{1,0:T(8,128)(2,1)S(1)}, bf16[32,7296]{1,0:T(8,128)(2,1)S(1)}, u32[]{:S(2)}, u32[]{:S(2)}) collective-permute-start(bf16[32,7296]{1,0:T(8,128)(2,1)S(1)} %reshape.10.after_ref.mine_in), channel_id=1, source_target_pairs={{0,8},{1,25},{2,10},{3,27},{4,12},{5,29},{6,14},{7,31},{8,16},{9,1... | collective-permute-start | bytes 1400840 | tf_op jit(solution)/shard_map/ppermute | solution.py:139
  24.1 9.8 %collective-permute-start.6 = (bf16[32,7296]{1,0:T(8,128)(2,1)S(1)}, bf16[32,7296]{1,0:T(8,128)(2,1)S(1)}, u32[]{:S(2)}, u32[]{:S(2)}) collective-permute-start(bf16[32,7296]{1,0:T(8,128)(2,1)S(1)} %reshape.10.after_ref.mine_in), channel_id=1, source_target_pairs={{0,2},{1,7},{2,4},{3,1},{4,6},{5,3},{6,0},{7,5},{8,10},{9,15},{10,... | collective-permute-start | bytes 1400840 | tf_op jit(solution)/shard_map/ppermute | solution.py:139
  24.9 13.7 %collective-permute-start.10 = (bf16[32,7296]{1,0:T(8,128)(2,1)S(1)}, bf16[32,7296]{1,0:T(8,128)(2,1)S(1)}, u32[]{:S(2)}, u32[]{:S(2)}) collective-permute-start(bf16[32,7296]{1,0:T(8,128)(2,1)S(1)} %reshape.10.after_ref.mine_in), channel_id=1, source_target_pairs={{0,32},{1,97},{2,34},{3,99},{4,36},{5,101},{6,38},{7,103},{8,40},{... | collective-permute-start | bytes 1400840 | tf_op jit(solution)/shard_map/ppermute | solution.py:139
  24.9 13.9 %collective-permute-start = (bf16[32,7296]{1,0:T(8,128)(2,1)S(1)}, bf16[32,7296]{1,0:T(8,128)(2,1)S(1)}, u32[]{:S(2)}, u32[]{:S(2)}) collective-permute-start(bf16[32,7296]{1,0:T(8,128)(2,1)S(1)} %reshape.10.after_ref.mine_in), channel_id=1, source_target_pairs={{0,1},{1,0},{2,3},{3,2},{4,5},{5,4},{6,7},{7,6},{8,9},{9,8},{10,11... | collective-permute-start | bytes 1400840 | tf_op jit(solution)/shard_map/ppermute | solution.py:139
  33.9 7.1 %collective-permute-start.3 = (bf16[32,7296]{1,0:T(8,128)(2,1)S(1)}, bf16[32,7296]{1,0:T(8,128)(2,1)S(1)}, u32[]{:S(2)}, u32[]{:S(2)}) collective-permute-start(bf16[32,7296]{1,0:T(8,128)(2,1)S(1)} %collective-permute-done.2.mine_in), channel_id=1, source_target_pairs={{0,1},{1,0},{2,3},{3,2},{4,5},{5,4},{6,7},{7,6},{8,9},{9,8},{10,11... | collective-permute-start | bytes 1400840 | tf_op jit(solution)/shard_map/ppermute | solution.py:139
  33.9 9.8 %collective-permute-start.7 = (bf16[32,7296]{1,0:T(8,128)(2,1)S(1)}, bf16[32,7296]{1,0:T(8,128)(2,1)S(1)}, u32[]{:S(2)}, u32[]{:S(2)}) collective-permute-start(bf16[32,7296]{1,0:T(8,128)(2,1)S(1)} %collective-permute-done.6.mine_in), channel_id=1, source_target_pairs={{0,1},{1,0},{2,3},{3,2},{4,5},{5,4},{6,7},{7,6},{8,9},{9,8},{10,11... | collective-permute-start | bytes 1400840 | tf_op jit(solution)/shard_map/ppermute | solution.py:139
  38.6 7.7 %collective-permute-start.11 = (bf16[32,7296]{1,0:T(8,128)(2,1)S(1)}, bf16[32,7296]{1,0:T(8,128)(2,1)S(1)}, u32[]{:S(2)}, u32[]{:S(2)}) collective-permute-start(bf16[32,7296]{1,0:T(8,128)(2,1)S(1)} %collective-permute-done.10.mine_in), channel_id=1, source_target_pairs={{0,1},{1,0},{2,3},{3,2},{4,5},{5,4},{6,7},{7,6},{8,9},{9,8},{10,11... | collective-permute-start | bytes 1400840 | tf_op jit(solution)/shard_map/ppermute | solution.py:139
  43.1 5.6 %collective-permute-start.4 = (bf16[32,7168]{1,0:T(8,128)(2,1)S(1)}, bf16[32,7168]{1,0:T(8,128)(2,1)S(1)}, u32[]{:S(2)}, u32[]{:S(2)}) collective-permute-start(bf16[32,7168]{1,0:T(8,128)(2,1)S(1)} %get-tuple-element.22.after_ref), channel_id=1, source_target_pairs={{0,1},{1,0},{2,3},{3,2},{4,5},{5,4},{6,7},{7,6},{8,9},{9,8},{10,11... | collective-permute-start | bytes 1376264 | tf_op jit(solution)/shard_map/ppermute | solution.py:139
  43.6 9.9 %collective-permute-start.1 = (bf16[32,7168]{1,0:T(8,128)(2,1)S(1)}, bf16[32,7168]{1,0:T(8,128)(2,1)S(1)}, u32[]{:S(2)}, u32[]{:S(2)}) collective-permute-start(bf16[32,7168]{1,0:T(8,128)(2,1)S(1)} %get-tuple-element.20.after_ref), channel_id=1, source_target_pairs={{0,1},{1,0},{2,3},{3,2},{4,5},{5,4},{6,7},{7,6},{8,9},{9,8},{10,11... | collective-permute-start | bytes 1376264 | tf_op jit(solution)/shard_map/ppermute | solution.py:139
  45.8 6.1 %collective-permute-start.8 = (bf16[32,7168]{1,0:T(8,128)(2,1)S(1)}, bf16[32,7168]{1,0:T(8,128)(2,1)S(1)}, u32[]{:S(2)}, u32[]{:S(2)}) collective-permute-start(bf16[32,7168]{1,0:T(8,128)(2,1)S(1)} %get-tuple-element.24.after_ref), channel_id=1, source_target_pairs={{0,1},{1,0},{2,3},{3,2},{4,5},{5,4},{6,7},{7,6},{8,9},{9,8},{10,11... | collective-permute-start | bytes 1376264 | tf_op jit(solution)/shard_map/ppermute | solution.py:139
  48.5 3.7 %collective-permute-start.12 = (bf16[32,7168]{1,0:T(8,128)(2,1)S(1)}, bf16[32,7168]{1,0:T(8,128)(2,1)S(1)}, u32[]{:S(2)}, u32[]{:S(2)}) collective-permute-start(bf16[32,7168]{1,0:T(8,128)(2,1)S(1)} %get-tuple-element.26), channel_id=1, source_target_pairs={{0,1},{1,0},{2,3},{3,2},{4,5},{5,4},{6,7},{7,6},{8,9},{9,8},{10,11... | collective-permute-start | bytes 1376264 | tf_op jit(solution)/shard_map/ppermute | solution.py:139
  48.7 9.2 %collective-permute-start.5 = (bf16[32,7168]{1,0:T(8,128)(2,1)S(1)}, bf16[32,7168]{1,0:T(8,128)(2,1)S(1)}, u32[]{:S(2)}, u32[]{:S(2)}) collective-permute-start(bf16[32,7168]{1,0:T(8,128)(2,1)S(1)} %add_convert_fusion.3), channel_id=1, source_target_pairs={{8,0},{25,1},{10,2},{27,3},{12,4},{29,5},{14,6},{31,7},{16,8},{1,9... | collective-permute-start | bytes 1376264 | tf_op jit(solution)/shard_map/ppermute | solution.py:139
  52.0 8.5 %collective-permute-start.9 = (bf16[32,7168]{1,0:T(8,128)(2,1)S(1)}, bf16[32,7168]{1,0:T(8,128)(2,1)S(1)}, u32[]{:S(2)}, u32[]{:S(2)}) collective-permute-start(bf16[32,7168]{1,0:T(8,128)(2,1)S(1)} %add_convert_fusion.2), channel_id=1, source_target_pairs={{2,0},{7,1},{4,2},{1,3},{6,4},{3,5},{0,6},{5,7},{10,8},{15,9},{12,... | collective-permute-start | bytes 1376264 | tf_op jit(solution)/shard_map/ppermute | solution.py:139
  52.2 8.5 %collective-permute-start.13 = (bf16[32,7168]{1,0:T(8,128)(2,1)S(1)}, bf16[32,7168]{1,0:T(8,128)(2,1)S(1)}, u32[]{:S(2)}, u32[]{:S(2)}) collective-permute-start(bf16[32,7168]{1,0:T(8,128)(2,1)S(1)} %add_convert_fusion.1), channel_id=1, source_target_pairs={{32,0},{97,1},{34,2},{99,3},{36,4},{101,5},{38,6},{103,7},{40,8},{... | collective-permute-start | bytes 1376264 | tf_op jit(solution)/shard_map/ppermute | solution.py:139
where the time goes:
time: 79.2 us; the launch traced here: 79 us
  blocking collectives  39.6 us (50%)
  waiting for transfers between devices  16.3 us (21%)
  Pallas kernels  13.7 us (17%)
  starting transfers between devices  7.31 us (9%)
  other arithmetic  1.57 us (2%)
    all_to_all x1, blocking collectives, step(): lax.all_to_all(tiled, ALL, split_axis=0, concat_axis=0, axis_index_groups...  22.9 us
    all_to_all x1, blocking collectives, step(): lax.all_to_all(pieces, ALL, split_axis=0, concat_axis=0, axis_index_group...  16.7 us
    ppermute x14, waiting for transfers between devices, moved(): return lax.ppermute(block, ALL, pairs)  16.3 us
    pallas_call x4, Pallas kernels, run_experts(): pl.pallas_call(experts_kernel, out_shape=(jax.ShapeDtypeStruct((size, wid...  8.54 us
    ppermute x14, starting transfers between devices, moved(): return lax.ppermute(block, ALL, pairs)  7.31 us
    pallas_call x1, Pallas kernels, step(): pl.pallas_call(load_kernel, out_shape=[jax.ShapeDtypeStruct(w.shape[1:],...  4.23 us
  transfers between devices with their start and end apart: 14, of which 5 were waited for; matrix products, arithmetic and copies ran while one was open for 0% of the time, Pallas kernels for 16%

commit v1 on v0

--- a/solution.py
+++ b/solution.py
@@ -78,12 +78,13 @@
         copy.wait()
 
 
-def experts_kernel(me_ref, mine_in, theirs_in, wg, wu, wd, after_ref, mine_out, theirs_out, hid):
+def experts_kernel(me_ref, *refs):
+    ins, (wg, wu, wd, after_ref), outs, hid = refs[:4], refs[4:8], refs[8:12], refs[12]
     width = wg.shape[0]
-    size = mine_in.shape[0]
+    size = ins[0].shape[0]
 
     def rows(ks):
-        return jnp.concatenate([mine_in[:, ks], theirs_in[:, ks]], axis=0)
+        return jnp.concatenate([r[:, ks] for r in ins], axis=0)
 
     scores = rows(pl.ds(width, LANES)).astype(jnp.float32)
     lane = lax.broadcasted_iota(jnp.int32, scores.shape, 1)
@@ -100,25 +101,24 @@
     for i in range(width // KCH):
         ks = pl.ds(i * KCH, KCH)
         out = jnp.dot(hid[...], wd[:, ks], preferred_element_type=jnp.float32) * weight
-        mine_out[:, ks] = out[:size]
-        theirs_out[:, ks] = out[size:].astype(jnp.bfloat16)
+        for j, ref in enumerate(outs):
+            ref[:, ks] = out[j * size:(j + 1) * size].astype(ref.dtype)
 
 
 def run_experts(me, mine, theirs, weights, after):
-    size = mine.shape[0]
+    size = mine[0].shape[0]
     width, hidden = weights[0].shape
-    return pl.pallas_call(
+    kinds = [jnp.float32] * 2 + [jnp.bfloat16] * 2
+    outs = pl.pallas_call(
         experts_kernel,
-        out_shape=(
-            jax.ShapeDtypeStruct((size, width), jnp.float32),
-            jax.ShapeDtypeStruct((size, width), jnp.bfloat16),
-        ),
-        in_specs=[SMEM] + [VMEM] * 5 + [pl.BlockSpec(memory_space=pl.ANY)],
-        out_specs=(VMEM, VMEM),
-        scratch_shapes=[pltpu.VMEM((2 * size, hidden), jnp.bfloat16)],
+        out_shape=[jax.ShapeDtypeStruct((size, width), kind) for kind in kinds],
+        in_specs=[SMEM] + [VMEM] * 7 + [pl.BlockSpec(memory_space=pl.ANY)],
+        out_specs=[VMEM] * 4,
+        scratch_shapes=[pltpu.VMEM((4 * size, hidden), jnp.bfloat16)],
         compiler_params=LIMIT,
-        cost_estimate=cost(1.0),
-    )(me, mine, theirs, *weights, after)
+        cost_estimate=cost(1.8),
+    )(me, *mine, *theirs, *weights, after)
+    return outs[:2], outs[2:]
 
 
 VMEM = pl.BlockSpec(memory_space=pltpu.VMEM)
@@ -178,10 +178,11 @@
     swapped = {a: moved(b, swap_pairs()) for a, b in near.items()}
     total = {}
     after = me
-    for a in "oxyz":
-        mine, theirs = run_experts(me, near[a], swapped[a], (wg, wu, wd), after)
-        after = theirs
-        total[a] = mine + moved(theirs, swap_pairs()).astype(f32)
+    for pair in ("xo", "yz"):
+        mine, theirs = run_experts(me, [near[a] for a in pair], [swapped[a] for a in pair], (wg, wu, wd), after)
+        after = theirs[0]
+        for a, kept, sent in zip(pair, mine, theirs):
+            total[a] = kept + moved(sent, swap_pairs()).astype(f32)
     acc = total["o"]
     for a in "xyz":
         acc = acc + moved(total[a].astype(bf16), neighbour_pairs(a, True)).astype(f32)

time: 79.2 us -> 75.3 us (0.951)
  Pallas kernels: 13.7 us -> 8.68 us
  blocking collectives: 39.6 us -> 38.1 us
  waiting for transfers between devices: 16.3 us -> 17.8 us
  starting transfers between devices: 7.31 us -> 8.44 us
    pallas_call x4 -> x2, Pallas kernels: 8.54 us -> 3.55 us  [run_experts(): pl.pallas_call(experts_kernel, out_shape=[jax.ShapeDtypeStruct((size, wid...]
    all_to_all x1, blocking collectives: 16.7 us -> 15.2 us  [step(): lax.all_to_all(pieces, ALL, split_axis=0, concat_axis=0, axis_index_group...]
    ppermute x14, waiting for transfers between devices: 16.3 us -> 17.8 us  [moved(): return lax.ppermute(block, ALL, pairs)]
    ppermute x14, starting transfers between devices: 7.31 us -> 8.44 us  [moved(): return lax.ppermute(block, ALL, pairs)]
  transfers between devices with their start and end apart: 14 -> 14, of which waited for: 5 -> 6; matrix products, arithmetic and copies ran while one was open for 0% -> 0% of each run, Pallas kernels for 16% -> 10%
where the time goes in v1:
time: 75.3 us; the launch traced here: 75 us
  blocking collectives  38.1 us (51%)
  waiting for transfers between devices  17.8 us (24%)
  Pallas kernels  8.68 us (12%)
  starting transfers between devices  8.44 us (11%)
  other arithmetic  1.54 us (2%)
    all_to_all x1, blocking collectives, step(): lax.all_to_all(tiled, ALL, split_axis=0, concat_axis=0, axis_index_groups...  22.9 us
    ppermute x14, waiting for transfers between devices, moved(): return lax.ppermute(block, ALL, pairs)  17.8 us
    all_to_all x1, blocking collectives, step(): lax.all_to_all(pieces, ALL, split_axis=0, concat_axis=0, axis_index_group...  15.2 us
    ppermute x14, starting transfers between devices, moved(): return lax.ppermute(block, ALL, pairs)  8.44 us
    pallas_call x1, Pallas kernels, step(): pl.pallas_call(load_kernel, out_shape=[jax.ShapeDtypeStruct(w.shape[1:],...  4.23 us
    pallas_call x2, Pallas kernels, run_experts(): pl.pallas_call(experts_kernel, out_shape=[jax.ShapeDtypeStruct((size, wid...  3.55 us
  transfers between devices with their start and end apart: 14, of which 6 were waited for; matrix products, arithmetic and copies ran while one was open for 0% of the time, Pallas kernels for 10%

profile of v1, /device:TPU:0, one launch (start us, length us, event | category | flops | bytes accessed | tf_op | source)
XLA Modules:
  0.0 75.0 jit_solution(8399414218509823049)
XLA Ops:
  0.0 0.9 %head.1 = bf16[16,2,7296]{2,1,0:T(2,128)(2,1)S(1)} custom-call(s32[1]{0:T(128)} %bitcast.me_ref.refs_7_, bf16[2,7168]{1,0:T(2,128)(2,1)} %tok_hbm.1, s32[2,8]{1,0:T(2,128)} %ids_hbm.1, s32[2,8]{1,0:T(2,128)} %ints_hbm.1), custom_call_target="tpu_custom_call" | custom-call | tf_op jit(solution)/shard_map/head/pallas_call | solution.py:149
  0.9 22.9 %all_to_all.10 = bf16[16,2,7296]{2,1,0:T(2,128)(2,1)S(1)} all-to-all(bf16[16,2,7296]{2,1,0:T(2,128)(2,1)S(1)} %head.1), channel_id=1, replica_groups={{0,18,4,22,40,58,44,62,80,66,84,70,120,106,124,110},{1,19,5,23,41,59,45..., dimensions={0} | all-to-all | bytes 933888 | tf_op jit(solution)/shard_map/all_to_all | solution.py:163
  23.8 0.2 reshape.10.after_ref.refs_1_
  24.0 0.1 collective-permute-start
  24.1 0.8 %collective-permute-start.6 = (bf16[32,7296]{1,0:T(8,128)(2,1)S(1)}, bf16[32,7296]{1,0:T(8,128)(2,1)S(1)}, u32[]{:S(2)}, u32[]{:S(2)}) collective-permute-start(bf16[32,7296]{1,0:T(8,128)(2,1)S(1)} %reshape.10.after_ref.refs_1_), channel_id=1, source_target_pairs={{0,2},{1,7},{2,4},{3,1},{4,6},{5,3},{6,0},{7,5},{8,10},{9,15},{10,... | collective-permute-start | bytes 1400840 | tf_op jit(solution)/shard_map/ppermute | solution.py:139
  24.9 8.9 %collective-permute-done.refs_0_ = bf16[32,7296]{1,0:T(8,128)(2,1)S(1)} collective-permute-done((bf16[32,7296]{1,0:T(8,128)(2,1)S(1)}, bf16[32,7296]{1,0:T(8,128)(2,1)S(1)}, u32[]{:S(2)}, u32[]{:S(2)}) %collective-permute-start) | collective-permute-done | bytes 466976 | tf_op jit(solution)/shard_map/ppermute | solution.py:139
  33.9 0.0 collective-permute-start.1
  33.9 0.1 collective-permute-done.6.refs_0_
  33.9 0.4 collective-permute-start.8
  34.4 0.3 collective-permute-done.7.refs_1_
  34.7 4.2 %load.1 = (bf16[7168,256]{1,0:T(8,128)(2,1)S(1)}, bf16[7168,256]{1,0:T(8,128)(2,1)S(1)}, bf16[256,7168]{1,0:T(8,128)(2,1)S(1)}) custom-call(bf16[7168,256]{1,0:T(8,128)(2,1)} %bitcast.4, bf16[7168,256]{1,0:T(8,128)(2,1)} %bitcast.5, bf16[256,7168]{1,0:T(8,128)(2,1)} %bitcast.6, bf16[32,7296]{1,0:T(8,128)(2,1)S(1)} %reshape.10.after_ref.refs_1_), custom_call_target="tpu_custom_call" | custom-call | flops 850000000 | tf_op jit(solution)/shard_map/load/pallas_call | solution.py:165
  38.9 0.0 collective-permute-done.1.refs_2_
  38.9 1.8 %shard_map.64 = (f32[32,7168]{1,0:T(8,128)S(1)}, f32[32,7168]{1,0:T(8,128)S(1)}, bf16[32,7168]{1,0:T(8,128)(2,1)S(1)}, bf16[32,7168]{1,0:T(8,128)(2,1)S(1)}) custom-call(s32[1]{0:T(128)} %bitcast.me_ref.refs_7_, bf16[32,7296]{1,0:T(8,128)(2,1)S(1)} %collective-permute-done.refs_0_, bf16[32,7296]{1,0:T(8,128)(2,1)S(1)} %reshape.10.after_ref.refs_1_, ...), custom_call_target="tpu_custom_call" | custom-call | flops 450000000 | tf_op jit(solution)/shard_map/pallas_call | solution.py:112
  40.7 0.6 collective-permute-start.4
  41.3 0.0 collective-permute-done.8.refs_2_
  41.3 1.8 %shard_map.65 = (f32[32,7168]{1,0:T(8,128)S(1)}, f32[32,7168]{1,0:T(8,128)S(1)}, bf16[32,7168]{1,0:T(8,128)(2,1)S(1)}, bf16[32,7168]{1,0:T(8,128)(2,1)S(1)}) custom-call(s32[1]{0:T(128)} %bitcast.me_ref.refs_7_, bf16[32,7296]{1,0:T(8,128)(2,1)S(1)} %collective-permute-done.6.refs_0_, bf16[32,7296]{1,0:T(8,128)(2,1)S(1)} %collective-permute-done.7.refs_1_, ...), custom_call_target="tpu_custom_call" | custom-call | flops 450000000 | tf_op jit(solution)/shard_map/pallas_call | solution.py:112
  43.1 0.1 collective-permute-start.10
  43.2 0.5 collective-permute-start.12
  43.7 0.1 collective-permute-start.3
  43.8 0.1 add_convert_fusion.3
  43.9 2.9 %collective-permute-start.5 = (bf16[32,7168]{1,0:T(8,128)(2,1)S(1)}, bf16[32,7168]{1,0:T(8,128)(2,1)S(1)}, u32[]{:S(2)}, u32[]{:S(2)}) collective-permute-start(bf16[32,7168]{1,0:T(8,128)(2,1)S(1)} %add_convert_fusion.3), channel_id=1, source_target_pairs={{8,0},{25,1},{10,2},{27,3},{12,4},{29,5},{14,6},{31,7},{16,8},{1,9... | collective-permute-start | bytes 1376264 | tf_op jit(solution)/shard_map/ppermute | solution.py:139
  46.8 0.1 add_convert_fusion.2
  46.9 2.9 %collective-permute-start.11 = (bf16[32,7168]{1,0:T(8,128)(2,1)S(1)}, bf16[32,7168]{1,0:T(8,128)(2,1)S(1)}, u32[]{:S(2)}, u32[]{:S(2)}) collective-permute-start(bf16[32,7168]{1,0:T(8,128)(2,1)S(1)} %add_convert_fusion.2), channel_id=1, source_target_pairs={{2,0},{7,1},{4,2},{1,3},{6,4},{3,5},{0,6},{5,7},{10,8},{15,9},{12,... | collective-permute-start | bytes 1376264 | tf_op jit(solution)/shard_map/ppermute | solution.py:139
  49.8 0.1 add_convert_fusion.1
  49.8 0.1 collective-permute-start.13
  49.9 2.9 %collective-permute-done.5 = bf16[32,7168]{1,0:T(8,128)(2,1)S(1)} collective-permute-done((bf16[32,7168]{1,0:T(8,128)(2,1)S(1)}, bf16[32,7168]{1,0:T(8,128)(2,1)S(1)}, u32[]{:S(2)}, u32[]{:S(2)}) %collective-permute-start.5) | collective-permute-done | bytes 458784 | tf_op jit(solution)/shard_map/ppermute | solution.py:139
  52.8 3.0 %collective-permute-done.11 = bf16[32,7168]{1,0:T(8,128)(2,1)S(1)} collective-permute-done((bf16[32,7168]{1,0:T(8,128)(2,1)S(1)}, bf16[32,7168]{1,0:T(8,128)(2,1)S(1)}, u32[]{:S(2)}, u32[]{:S(2)}) %collective-permute-start.11) | collective-permute-done | bytes 458784 | tf_op jit(solution)/shard_map/ppermute | solution.py:139
  55.8 2.6 %collective-permute-done.13 = bf16[32,7168]{1,0:T(8,128)(2,1)S(1)} collective-permute-done((bf16[32,7168]{1,0:T(8,128)(2,1)S(1)}, bf16[32,7168]{1,0:T(8,128)(2,1)S(1)}, u32[]{:S(2)}, u32[]{:S(2)}) %collective-permute-start.13) | collective-permute-done | bytes 458784 | tf_op jit(solution)/shard_map/ppermute | solution.py:139
  58.4 0.3 add_convert_fusion
  58.7 0.2 reshape.11
  58.9 15.2 %all_to_all.11 = bf16[16,2,7168]{2,1,0:T(2,128)(2,1)S(1)} all-to-all(bf16[16,2,7168]{2,1,0:T(2,128)(2,1)S(1)} %reshape.11), channel_id=1, replica_groups={{0,18,4,22,40,58,44,62,80,66,84,70,120,106,124,110},{1,19,5,23,41,59,45..., dimensions={0} | all-to-all | bytes 917504 | tf_op jit(solution)/shard_map/all_to_all | solution.py:190
  74.0 1.0 %reduce_sum.12 = bf16[2,7168]{1,0:T(2,128)(2,1)} reduce(bf16[16,2,7168]{2,1,0:T(2,128)(2,1)S(1)} %all_to_all.11, bf16[]{:T(256)} %constant.13.clone.1), dimensions={0}, to_apply=%region_0.0 | reduce | flops 215040 | bytes 487426 | tf_op jit(solution)/shard_map/reduce_sum | solution.py:191
  (9 shorter events, 0.0 us)
Async XLA Ops:
  24.0 9.8 %collective-permute-start = (bf16[32,7296]{1,0:T(8,128)(2,1)S(1)}, bf16[32,7296]{1,0:T(8,128)(2,1)S(1)}, u32[]{:S(2)}, u32[]{:S(2)}) collective-permute-start(bf16[32,7296]{1,0:T(8,128)(2,1)S(1)} %reshape.10.after_ref.refs_1_), channel_id=1, source_target_pairs={{0,8},{1,25},{2,10},{3,27},{4,12},{5,29},{6,14},{7,31},{8,16},{9,1... | collective-permute-start | bytes 1400840 | tf_op jit(solution)/shard_map/ppermute | solution.py:139
  24.1 9.8 %collective-permute-start.6 = (bf16[32,7296]{1,0:T(8,128)(2,1)S(1)}, bf16[32,7296]{1,0:T(8,128)(2,1)S(1)}, u32[]{:S(2)}, u32[]{:S(2)}) collective-permute-start(bf16[32,7296]{1,0:T(8,128)(2,1)S(1)} %reshape.10.after_ref.refs_1_), channel_id=1, source_target_pairs={{0,2},{1,7},{2,4},{3,1},{4,6},{5,3},{6,0},{7,5},{8,10},{9,15},{10,... | collective-permute-start | bytes 1400840 | tf_op jit(solution)/shard_map/ppermute | solution.py:139
  24.9 9.8 %collective-permute-start.7 = (bf16[32,7296]{1,0:T(8,128)(2,1)S(1)}, bf16[32,7296]{1,0:T(8,128)(2,1)S(1)}, u32[]{:S(2)}, u32[]{:S(2)}) collective-permute-start(bf16[32,7296]{1,0:T(8,128)(2,1)S(1)} %reshape.10.after_ref.refs_1_), channel_id=1, source_target_pairs={{0,32},{1,97},{2,34},{3,99},{4,36},{5,101},{6,38},{7,103},{8,40},{... | collective-permute-start | bytes 1400840 | tf_op jit(solution)/shard_map/ppermute | solution.py:139
  24.9 14.0 %collective-permute-start.2 = (bf16[32,7296]{1,0:T(8,128)(2,1)S(1)}, bf16[32,7296]{1,0:T(8,128)(2,1)S(1)}, u32[]{:S(2)}, u32[]{:S(2)}) collective-permute-start(bf16[32,7296]{1,0:T(8,128)(2,1)S(1)} %reshape.10.after_ref.refs_1_), channel_id=1, source_target_pairs={{0,1},{1,0},{2,3},{3,2},{4,5},{5,4},{6,7},{7,6},{8,9},{9,8},{10,11... | collective-permute-start | bytes 1400840 | tf_op jit(solution)/shard_map/ppermute | solution.py:139
  33.9 5.1 %collective-permute-start.1 = (bf16[32,7296]{1,0:T(8,128)(2,1)S(1)}, bf16[32,7296]{1,0:T(8,128)(2,1)S(1)}, u32[]{:S(2)}, u32[]{:S(2)}) collective-permute-start(bf16[32,7296]{1,0:T(8,128)(2,1)S(1)} %collective-permute-done.refs_0_), channel_id=1, source_target_pairs={{0,1},{1,0},{2,3},{3,2},{4,5},{5,4},{6,7},{7,6},{8,9},{9,8},{10,11... | collective-permute-start | bytes 1400840 | tf_op jit(solution)/shard_map/ppermute | solution.py:139
  33.9 7.4 %collective-permute-start.8 = (bf16[32,7296]{1,0:T(8,128)(2,1)S(1)}, bf16[32,7296]{1,0:T(8,128)(2,1)S(1)}, u32[]{:S(2)}, u32[]{:S(2)}) collective-permute-start(bf16[32,7296]{1,0:T(8,128)(2,1)S(1)} %collective-permute-done.6.refs_0_), channel_id=1, source_target_pairs={{0,1},{1,0},{2,3},{3,2},{4,5},{5,4},{6,7},{7,6},{8,9},{9,8},{10,11... | collective-permute-start | bytes 1400840 | tf_op jit(solution)/shard_map/ppermute | solution.py:139
  34.7 6.6 %collective-permute-start.9 = (bf16[32,7296]{1,0:T(8,128)(2,1)S(1)}, bf16[32,7296]{1,0:T(8,128)(2,1)S(1)}, u32[]{:S(2)}, u32[]{:S(2)}) collective-permute-start(bf16[32,7296]{1,0:T(8,128)(2,1)S(1)} %collective-permute-done.7.refs_1_), channel_id=1, source_target_pairs={{0,1},{1,0},{2,3},{3,2},{4,5},{5,4},{6,7},{7,6},{8,9},{9,8},{10,11... | collective-permute-start | bytes 1400840 | tf_op jit(solution)/shard_map/ppermute | solution.py:139
  40.7 3.0 %collective-permute-start.4 = (bf16[32,7168]{1,0:T(8,128)(2,1)S(1)}, bf16[32,7168]{1,0:T(8,128)(2,1)S(1)}, u32[]{:S(2)}, u32[]{:S(2)}) collective-permute-start(bf16[32,7168]{1,0:T(8,128)(2,1)S(1)} %get-tuple-element.22.refs_7_), channel_id=1, source_target_pairs={{0,1},{1,0},{2,3},{3,2},{4,5},{5,4},{6,7},{7,6},{8,9},{9,8},{10,11... | collective-permute-start | bytes 1376264 | tf_op jit(solution)/shard_map/ppermute | solution.py:139
  43.1 3.7 %collective-permute-start.10 = (bf16[32,7168]{1,0:T(8,128)(2,1)S(1)}, bf16[32,7168]{1,0:T(8,128)(2,1)S(1)}, u32[]{:S(2)}, u32[]{:S(2)}) collective-permute-start(bf16[32,7168]{1,0:T(8,128)(2,1)S(1)} %get-tuple-element.24), channel_id=1, source_target_pairs={{0,1},{1,0},{2,3},{3,2},{4,5},{5,4},{6,7},{7,6},{8,9},{9,8},{10,11... | collective-permute-start | bytes 1376264 | tf_op jit(solution)/shard_map/ppermute | solution.py:139
  43.2 6.6 %collective-permute-start.12 = (bf16[32,7168]{1,0:T(8,128)(2,1)S(1)}, bf16[32,7168]{1,0:T(8,128)(2,1)S(1)}, u32[]{:S(2)}, u32[]{:S(2)}) collective-permute-start(bf16[32,7168]{1,0:T(8,128)(2,1)S(1)} %get-tuple-element.26), channel_id=1, source_target_pairs={{0,1},{1,0},{2,3},{3,2},{4,5},{5,4},{6,7},{7,6},{8,9},{9,8},{10,11... | collective-permute-start | bytes 1376264 | tf_op jit(solution)/shard_map/ppermute | solution.py:139
  43.7 6.3 %collective-permute-start.3 = (bf16[32,7168]{1,0:T(8,128)(2,1)S(1)}, bf16[32,7168]{1,0:T(8,128)(2,1)S(1)}, u32[]{:S(2)}, u32[]{:S(2)}) collective-permute-start(bf16[32,7168]{1,0:T(8,128)(2,1)S(1)} %get-tuple-element.20), channel_id=1, source_target_pairs={{0,1},{1,0},{2,3},{3,2},{4,5},{5,4},{6,7},{7,6},{8,9},{9,8},{10,11... | collective-permute-start | bytes 1376264 | tf_op jit(solution)/shard_map/ppermute | solution.py:139
  43.9 8.9 %collective-permute-start.5 = (bf16[32,7168]{1,0:T(8,128)(2,1)S(1)}, bf16[32,7168]{1,0:T(8,128)(2,1)S(1)}, u32[]{:S(2)}, u32[]{:S(2)}) collective-permute-start(bf16[32,7168]{1,0:T(8,128)(2,1)S(1)} %add_convert_fusion.3), channel_id=1, source_target_pairs={{8,0},{25,1},{10,2},{27,3},{12,4},{29,5},{14,6},{31,7},{16,8},{1,9... | collective-permute-start | bytes 1376264 | tf_op jit(solution)/shard_map/ppermute | solution.py:139
  46.9 8.9 %collective-permute-start.11 = (bf16[32,7168]{1,0:T(8,128)(2,1)S(1)}, bf16[32,7168]{1,0:T(8,128)(2,1)S(1)}, u32[]{:S(2)}, u32[]{:S(2)}) collective-permute-start(bf16[32,7168]{1,0:T(8,128)(2,1)S(1)} %add_convert_fusion.2), channel_id=1, source_target_pairs={{2,0},{7,1},{4,2},{1,3},{6,4},{3,5},{0,6},{5,7},{10,8},{15,9},{12,... | collective-permute-start | bytes 1376264 | tf_op jit(solution)/shard_map/ppermute | solution.py:139
  49.8 8.5 %collective-permute-start.13 = (bf16[32,7168]{1,0:T(8,128)(2,1)S(1)}, bf16[32,7168]{1,0:T(8,128)(2,1)S(1)}, u32[]{:S(2)}, u32[]{:S(2)}) collective-permute-start(bf16[32,7168]{1,0:T(8,128)(2,1)S(1)} %add_convert_fusion.1), channel_id=1, source_target_pairs={{32,0},{97,1},{34,2},{99,3},{36,4},{101,5},{38,6},{103,7},{40,8},{... | collective-permute-start | bytes 1376264 | tf_op jit(solution)/shard_map/ppermute | solution.py:139

commit v2 on v1

--- a/solution.py
+++ b/solution.py
@@ -21,23 +21,22 @@
 
 def class_groups():
     groups = []
-    for colour in range(RING):
-        for c in range(2):
-            members = []
-            for z, y in itertools.product(range(RING), repeat=2):
-                members.append(index(z, (colour + 2 * y + z) % RING, y, c))
-            groups.append(members)
+    for a, b, c in itertools.product(range(2), repeat=3):
+        members = []
+        for z, x, y in itertools.product(range(RING), repeat=3):
+            if (x + z) % 2 == a and (y + z) % 2 == b:
+                members.append(index(z, x, y, c))
+        groups.append(members)
     return groups
 
 
-def neighbour_pairs(axis, back):
+def neighbour_pairs(axis):
     pairs = []
     for z, x, y in itertools.product(range(RING), repeat=3):
         for c in range(2):
             there = {"z": z, "x": x, "y": y}
-            there[axis] = (there[axis] + (1 if c == 0 else -1)) % RING
-            pair = (index(z, x, y, c), index(there["z"], there["x"], there["y"], c))
-            pairs.append(pair[::-1] if back else pair)
+            there[axis] = RING - 1 - there[axis] if c else there[axis] ^ 1
+            pairs.append((index(z, x, y, c), index(there["z"], there["x"], there["y"], c)))
     return pairs
 
 
@@ -173,7 +172,7 @@
         name="load",
     )(*in_hbm(w_gate[0], w_up[0], w_down[0]), own)
 
-    near = {a: moved(own, neighbour_pairs(a, False)) for a in "xyz"}
+    near = {a: moved(own, neighbour_pairs(a)) for a in "xyz"}
     near["o"] = own
     swapped = {a: moved(b, swap_pairs()) for a, b in near.items()}
     total = {}
@@ -185,7 +184,7 @@
             total[a] = kept + moved(sent, swap_pairs()).astype(f32)
     acc = total["o"]
     for a in "xyz":
-        acc = acc + moved(total[a].astype(bf16), neighbour_pairs(a, True)).astype(f32)
+        acc = acc + moved(total[a].astype(bf16), neighbour_pairs(a)).astype(f32)
     pieces = acc.astype(bf16).reshape(n, tokens.shape[0], width)
     got = lax.all_to_all(pieces, ALL, split_axis=0, concat_axis=0, axis_index_groups=groups, tiled=True)
     return jnp.sum(got.astype(f32), axis=0).astype(bf16)

time: 75.3 us -> 74.3 us (0.987)
  blocking collectives: 38.1 us -> 40.6 us
  starting transfers between devices: 8.44 us -> 6.08 us
  waiting for transfers between devices: 17.8 us -> 16.6 us
    ppermute x14, starting transfers between devices: 8.44 us -> 6.08 us  [moved(): return lax.ppermute(block, ALL, pairs)]
    all_to_all x1, blocking collectives: 15.2 us -> 17.4 us  [step(): lax.all_to_all(pieces, ALL, split_axis=0, concat_axis=0, axis_index_group...]
    ppermute x14, waiting for transfers between devices: 17.8 us -> 16.6 us  [moved(): return lax.ppermute(block, ALL, pairs)]
where the time goes in v2:
time: 74.3 us; the launch traced here: 74 us
  blocking collectives  40.6 us (55%)
  waiting for transfers between devices  16.6 us (22%)
  Pallas kernels  8.67 us (12%)
  starting transfers between devices  6.08 us (8%)
  other arithmetic  1.54 us (2%)
    all_to_all x1, blocking collectives, step(): lax.all_to_all(tiled, ALL, split_axis=0, concat_axis=0, axis_index_groups...  23.2 us
    all_to_all x1, blocking collectives, step(): lax.all_to_all(pieces, ALL, split_axis=0, concat_axis=0, axis_index_group...  17.4 us
    ppermute x14, waiting for transfers between devices, moved(): return lax.ppermute(block, ALL, pairs)  16.6 us
    ppermute x14, starting transfers between devices, moved(): return lax.ppermute(block, ALL, pairs)  6.08 us
    pallas_call x1, Pallas kernels, step(): pl.pallas_call(load_kernel, out_shape=[jax.ShapeDtypeStruct(w.shape[1:],...  4.23 us
    pallas_call x2, Pallas kernels, run_experts(): pl.pallas_call(experts_kernel, out_shape=[jax.ShapeDtypeStruct((size, wid...  3.54 us
  transfers between devices with their start and end apart: 14, of which 6 were waited for; matrix products, arithmetic and copies ran while one was open for 0% of the time, Pallas kernels for 10%

profile of v2, /device:TPU:0, one launch (start us, length us, event | category | flops | bytes accessed | tf_op | source)
XLA Modules:
  0.0 74.0 jit_solution(13029251671021883350)
XLA Ops:
  0.0 0.9 %head.1 = bf16[16,2,7296]{2,1,0:T(2,128)(2,1)S(1)} custom-call(s32[1]{0:T(128)} %bitcast.me_ref.refs_7_, bf16[2,7168]{1,0:T(2,128)(2,1)} %tok_hbm.1, s32[2,8]{1,0:T(2,128)} %ids_hbm.1, s32[2,8]{1,0:T(2,128)} %ints_hbm.1), custom_call_target="tpu_custom_call" | custom-call | tf_op jit(solution)/shard_map/head/pallas_call | solution.py:148
  0.9 23.2 %all_to_all.10 = bf16[16,2,7296]{2,1,0:T(2,128)(2,1)S(1)} all-to-all(bf16[16,2,7296]{2,1,0:T(2,128)(2,1)S(1)} %head.1), channel_id=1, replica_groups={{0,4,16,20,42,46,58,62,64,68,80,84,106,110,122,126},{1,5,17,21,43,47,59..., dimensions={0} | all-to-all | bytes 933888 | tf_op jit(solution)/shard_map/all_to_all | solution.py:162
  24.1 0.2 reshape.10.after_ref.refs_1_
  24.3 0.7 collective-permute-start
  25.0 0.7 collective-permute-start.6
  25.6 0.4 collective-permute-start.7
  26.1 0.0 collective-permute-start.2
  26.1 6.9 %collective-permute-done.refs_0_ = bf16[32,7296]{1,0:T(8,128)(2,1)S(1)} collective-permute-done((bf16[32,7296]{1,0:T(8,128)(2,1)S(1)}, bf16[32,7296]{1,0:T(8,128)(2,1)S(1)}, u32[]{:S(2)}, u32[]{:S(2)}) %collective-permute-start) | collective-permute-done | bytes 466976 | tf_op jit(solution)/shard_map/ppermute | solution.py:138
  33.0 0.6 collective-permute-done.6.refs_0_
  33.5 0.0 collective-permute-start.8
  33.5 0.7 collective-permute-done.7.refs_1_
  34.2 0.4 collective-permute-start.9
  34.7 4.2 %load.1 = (bf16[7168,256]{1,0:T(8,128)(2,1)S(1)}, bf16[7168,256]{1,0:T(8,128)(2,1)S(1)}, bf16[256,7168]{1,0:T(8,128)(2,1)S(1)}) custom-call(bf16[7168,256]{1,0:T(8,128)(2,1)} %bitcast.4, bf16[7168,256]{1,0:T(8,128)(2,1)} %bitcast.5, bf16[256,7168]{1,0:T(8,128)(2,1)} %bitcast.6, bf16[32,7296]{1,0:T(8,128)(2,1)S(1)} %reshape.10.after_ref.refs_1_), custom_call_target="tpu_custom_call" | custom-call | flops 850000000 | tf_op jit(solution)/shard_map/load/pallas_call | solution.py:164
  38.9 1.8 %shard_map.64 = (f32[32,7168]{1,0:T(8,128)S(1)}, f32[32,7168]{1,0:T(8,128)S(1)}, bf16[32,7168]{1,0:T(8,128)(2,1)S(1)}, bf16[32,7168]{1,0:T(8,128)(2,1)S(1)}) custom-call(s32[1]{0:T(128)} %bitcast.me_ref.refs_7_, bf16[32,7296]{1,0:T(8,128)(2,1)S(1)} %collective-permute-done.refs_0_, bf16[32,7296]{1,0:T(8,128)(2,1)S(1)} %reshape.10.after_ref.refs_1_, ...), custom_call_target="tpu_custom_call" | custom-call | flops 450000000 | tf_op jit(solution)/shard_map/pallas_call | solution.py:111
  40.7 0.1 collective-permute-start.4
  40.8 1.8 %shard_map.65 = (f32[32,7168]{1,0:T(8,128)S(1)}, f32[32,7168]{1,0:T(8,128)S(1)}, bf16[32,7168]{1,0:T(8,128)(2,1)S(1)}, bf16[32,7168]{1,0:T(8,128)(2,1)S(1)}) custom-call(s32[1]{0:T(128)} %bitcast.me_ref.refs_7_, bf16[32,7296]{1,0:T(8,128)(2,1)S(1)} %collective-permute-done.6.refs_0_, bf16[32,7296]{1,0:T(8,128)(2,1)S(1)} %collective-permute-done.7.refs_1_, ...), custom_call_target="tpu_custom_call" | custom-call | flops 450000000 | tf_op jit(solution)/shard_map/pallas_call | solution.py:111
  42.6 0.5 collective-permute-start.10
  43.2 0.1 collective-permute-start.12
  43.2 0.4 collective-permute-start.3
  43.7 0.1 add_convert_fusion.3
  43.8 1.2 %collective-permute-start.5 = (bf16[32,7168]{1,0:T(8,128)(2,1)S(1)}, bf16[32,7168]{1,0:T(8,128)(2,1)S(1)}, u32[]{:S(2)}, u32[]{:S(2)}) collective-permute-start(bf16[32,7168]{1,0:T(8,128)(2,1)S(1)} %add_convert_fusion.3), channel_id=1, source_target_pairs={{0,8},{1,25},{2,10},{3,27},{4,12},{5,29},{6,14},{7,31},{8,0},{9,17... | collective-permute-start | bytes 1376264 | tf_op jit(solution)/shard_map/ppermute | solution.py:138
  44.9 0.1 add_convert_fusion.2
  45.0 1.4 %collective-permute-start.11 = (bf16[32,7168]{1,0:T(8,128)(2,1)S(1)}, bf16[32,7168]{1,0:T(8,128)(2,1)S(1)}, u32[]{:S(2)}, u32[]{:S(2)}) collective-permute-start(bf16[32,7168]{1,0:T(8,128)(2,1)S(1)} %add_convert_fusion.2), channel_id=1, source_target_pairs={{0,2},{1,7},{2,0},{3,5},{4,6},{5,3},{6,4},{7,1},{8,10},{9,15},{10,... | collective-permute-start | bytes 1376264 | tf_op jit(solution)/shard_map/ppermute | solution.py:138
  46.5 0.1 add_convert_fusion.1
  46.5 0.1 collective-permute-start.13
  46.6 5.7 %collective-permute-done.5 = bf16[32,7168]{1,0:T(8,128)(2,1)S(1)} collective-permute-done((bf16[32,7168]{1,0:T(8,128)(2,1)S(1)}, bf16[32,7168]{1,0:T(8,128)(2,1)S(1)}, u32[]{:S(2)}, u32[]{:S(2)}) %collective-permute-start.5) | collective-permute-done | bytes 458784 | tf_op jit(solution)/shard_map/ppermute | solution.py:138
  52.3 1.2 %collective-permute-done.11 = bf16[32,7168]{1,0:T(8,128)(2,1)S(1)} collective-permute-done((bf16[32,7168]{1,0:T(8,128)(2,1)S(1)}, bf16[32,7168]{1,0:T(8,128)(2,1)S(1)}, u32[]{:S(2)}, u32[]{:S(2)}) %collective-permute-start.11) | collective-permute-done | bytes 458784 | tf_op jit(solution)/shard_map/ppermute | solution.py:138
  53.6 1.5 %collective-permute-done.13 = bf16[32,7168]{1,0:T(8,128)(2,1)S(1)} collective-permute-done((bf16[32,7168]{1,0:T(8,128)(2,1)S(1)}, bf16[32,7168]{1,0:T(8,128)(2,1)S(1)}, u32[]{:S(2)}, u32[]{:S(2)}) %collective-permute-start.13) | collective-permute-done | bytes 458784 | tf_op jit(solution)/shard_map/ppermute | solution.py:138
  55.1 0.3 add_convert_fusion
  55.4 0.2 reshape.11
  55.6 17.4 %all_to_all.11 = bf16[16,2,7168]{2,1,0:T(2,128)(2,1)S(1)} all-to-all(bf16[16,2,7168]{2,1,0:T(2,128)(2,1)S(1)} %reshape.11), channel_id=1, replica_groups={{0,4,16,20,42,46,58,62,64,68,80,84,106,110,122,126},{1,5,17,21,43,47,59..., dimensions={0} | all-to-all | bytes 917504 | tf_op jit(solution)/shard_map/all_to_all | solution.py:189
  73.0 1.0 %reduce_sum.12 = bf16[2,7168]{1,0:T(2,128)(2,1)} reduce(bf16[16,2,7168]{2,1,0:T(2,128)(2,1)S(1)} %all_to_all.11, bf16[]{:T(256)} %constant.13.clone.1), dimensions={0}, to_apply=%region_0.0 | reduce | flops 215040 | bytes 487426 | tf_op jit(solution)/shard_map/reduce_sum | solution.py:190
  (9 shorter events, 0.0 us)
Async XLA Ops:
  24.3 8.6 %collective-permute-start = (bf16[32,7296]{1,0:T(8,128)(2,1)S(1)}, bf16[32,7296]{1,0:T(8,128)(2,1)S(1)}, u32[]{:S(2)}, u32[]{:S(2)}) collective-permute-start(bf16[32,7296]{1,0:T(8,128)(2,1)S(1)} %reshape.10.after_ref.refs_1_), channel_id=1, source_target_pairs={{0,8},{1,25},{2,10},{3,27},{4,12},{5,29},{6,14},{7,31},{8,0},{9,17... | collective-permute-start | bytes 1400840 | tf_op jit(solution)/shard_map/ppermute | solution.py:138
  25.0 8.6 %collective-permute-start.6 = (bf16[32,7296]{1,0:T(8,128)(2,1)S(1)}, bf16[32,7296]{1,0:T(8,128)(2,1)S(1)}, u32[]{:S(2)}, u32[]{:S(2)}) collective-permute-start(bf16[32,7296]{1,0:T(8,128)(2,1)S(1)} %reshape.10.after_ref.refs_1_), channel_id=1, source_target_pairs={{0,2},{1,7},{2,0},{3,5},{4,6},{5,3},{6,4},{7,1},{8,10},{9,15},{10,... | collective-permute-start | bytes 1400840 | tf_op jit(solution)/shard_map/ppermute | solution.py:138
  25.6 8.6 %collective-permute-start.7 = (bf16[32,7296]{1,0:T(8,128)(2,1)S(1)}, bf16[32,7296]{1,0:T(8,128)(2,1)S(1)}, u32[]{:S(2)}, u32[]{:S(2)}) collective-permute-start(bf16[32,7296]{1,0:T(8,128)(2,1)S(1)} %reshape.10.after_ref.refs_1_), channel_id=1, source_target_pairs={{0,32},{1,97},{2,34},{3,99},{4,36},{5,101},{6,38},{7,103},{8,40},{... | collective-permute-start | bytes 1400840 | tf_op jit(solution)/shard_map/ppermute | solution.py:138
  26.1 12.8 %collective-permute-start.2 = (bf16[32,7296]{1,0:T(8,128)(2,1)S(1)}, bf16[32,7296]{1,0:T(8,128)(2,1)S(1)}, u32[]{:S(2)}, u32[]{:S(2)}) collective-permute-start(bf16[32,7296]{1,0:T(8,128)(2,1)S(1)} %reshape.10.after_ref.refs_1_), channel_id=1, source_target_pairs={{0,1},{1,0},{2,3},{3,2},{4,5},{5,4},{6,7},{7,6},{8,9},{9,8},{10,11... | collective-permute-start | bytes 1400840 | tf_op jit(solution)/shard_map/ppermute | solution.py:138
  32.9 6.0 %collective-permute-start.1 = (bf16[32,7296]{1,0:T(8,128)(2,1)S(1)}, bf16[32,7296]{1,0:T(8,128)(2,1)S(1)}, u32[]{:S(2)}, u32[]{:S(2)}) collective-permute-start(bf16[32,7296]{1,0:T(8,128)(2,1)S(1)} %collective-permute-done.refs_0_), channel_id=1, source_target_pairs={{0,1},{1,0},{2,3},{3,2},{4,5},{5,4},{6,7},{7,6},{8,9},{9,8},{10,11... | collective-permute-start | bytes 1400840 | tf_op jit(solution)/shard_map/ppermute | solution.py:138
  33.5 7.3 %collective-permute-start.8 = (bf16[32,7296]{1,0:T(8,128)(2,1)S(1)}, bf16[32,7296]{1,0:T(8,128)(2,1)S(1)}, u32[]{:S(2)}, u32[]{:S(2)}) collective-permute-start(bf16[32,7296]{1,0:T(8,128)(2,1)S(1)} %collective-permute-done.6.refs_0_), channel_id=1, source_target_pairs={{0,1},{1,0},{2,3},{3,2},{4,5},{5,4},{6,7},{7,6},{8,9},{9,8},{10,11... | collective-permute-start | bytes 1400840 | tf_op jit(solution)/shard_map/ppermute | solution.py:138
  34.2 6.6 %collective-permute-start.9 = (bf16[32,7296]{1,0:T(8,128)(2,1)S(1)}, bf16[32,7296]{1,0:T(8,128)(2,1)S(1)}, u32[]{:S(2)}, u32[]{:S(2)}) collective-permute-start(bf16[32,7296]{1,0:T(8,128)(2,1)S(1)} %collective-permute-done.7.refs_1_), channel_id=1, source_target_pairs={{0,1},{1,0},{2,3},{3,2},{4,5},{5,4},{6,7},{7,6},{8,9},{9,8},{10,11... | collective-permute-start | bytes 1400840 | tf_op jit(solution)/shard_map/ppermute | solution.py:138
  40.7 3.0 %collective-permute-start.4 = (bf16[32,7168]{1,0:T(8,128)(2,1)S(1)}, bf16[32,7168]{1,0:T(8,128)(2,1)S(1)}, u32[]{:S(2)}, u32[]{:S(2)}) collective-permute-start(bf16[32,7168]{1,0:T(8,128)(2,1)S(1)} %get-tuple-element.22.refs_7_), channel_id=1, source_target_pairs={{0,1},{1,0},{2,3},{3,2},{4,5},{5,4},{6,7},{7,6},{8,9},{9,8},{10,11... | collective-permute-start | bytes 1376264 | tf_op jit(solution)/shard_map/ppermute | solution.py:138
  42.6 2.3 %collective-permute-start.10 = (bf16[32,7168]{1,0:T(8,128)(2,1)S(1)}, bf16[32,7168]{1,0:T(8,128)(2,1)S(1)}, u32[]{:S(2)}, u32[]{:S(2)}) collective-permute-start(bf16[32,7168]{1,0:T(8,128)(2,1)S(1)} %get-tuple-element.24), channel_id=1, source_target_pairs={{0,1},{1,0},{2,3},{3,2},{4,5},{5,4},{6,7},{7,6},{8,9},{9,8},{10,11... | collective-permute-start | bytes 1376264 | tf_op jit(solution)/shard_map/ppermute | solution.py:138
  43.2 3.3 %collective-permute-start.12 = (bf16[32,7168]{1,0:T(8,128)(2,1)S(1)}, bf16[32,7168]{1,0:T(8,128)(2,1)S(1)}, u32[]{:S(2)}, u32[]{:S(2)}) collective-permute-start(bf16[32,7168]{1,0:T(8,128)(2,1)S(1)} %get-tuple-element.26), channel_id=1, source_target_pairs={{0,1},{1,0},{2,3},{3,2},{4,5},{5,4},{6,7},{7,6},{8,9},{9,8},{10,11... | collective-permute-start | bytes 1376264 | tf_op jit(solution)/shard_map/ppermute | solution.py:138
  43.2 3.4 %collective-permute-start.3 = (bf16[32,7168]{1,0:T(8,128)(2,1)S(1)}, bf16[32,7168]{1,0:T(8,128)(2,1)S(1)}, u32[]{:S(2)}, u32[]{:S(2)}) collective-permute-start(bf16[32,7168]{1,0:T(8,128)(2,1)S(1)} %get-tuple-element.20), channel_id=1, source_target_pairs={{0,1},{1,0},{2,3},{3,2},{4,5},{5,4},{6,7},{7,6},{8,9},{9,8},{10,11... | collective-permute-start | bytes 1376264 | tf_op jit(solution)/shard_map/ppermute | solution.py:138
  43.8 8.6 %collective-permute-start.5 = (bf16[32,7168]{1,0:T(8,128)(2,1)S(1)}, bf16[32,7168]{1,0:T(8,128)(2,1)S(1)}, u32[]{:S(2)}, u32[]{:S(2)}) collective-permute-start(bf16[32,7168]{1,0:T(8,128)(2,1)S(1)} %add_convert_fusion.3), channel_id=1, source_target_pairs={{0,8},{1,25},{2,10},{3,27},{4,12},{5,29},{6,14},{7,31},{8,0},{9,17... | collective-permute-start | bytes 1376264 | tf_op jit(solution)/shard_map/ppermute | solution.py:138
  45.0 8.6 %collective-permute-start.11 = (bf16[32,7168]{1,0:T(8,128)(2,1)S(1)}, bf16[32,7168]{1,0:T(8,128)(2,1)S(1)}, u32[]{:S(2)}, u32[]{:S(2)}) collective-permute-start(bf16[32,7168]{1,0:T(8,128)(2,1)S(1)} %add_convert_fusion.2), channel_id=1, source_target_pairs={{0,2},{1,7},{2,0},{3,5},{4,6},{5,3},{6,4},{7,1},{8,10},{9,15},{10,... | collective-permute-start | bytes 1376264 | tf_op jit(solution)/shard_map/ppermute | solution.py:138
  46.5 8.6 %collective-permute-start.13 = (bf16[32,7168]{1,0:T(8,128)(2,1)S(1)}, bf16[32,7168]{1,0:T(8,128)(2,1)S(1)}, u32[]{:S(2)}, u32[]{:S(2)}) collective-permute-start(bf16[32,7168]{1,0:T(8,128)(2,1)S(1)} %add_convert_fusion.1), channel_id=1, source_target_pairs={{0,32},{1,97},{2,34},{3,99},{4,36},{5,101},{6,38},{7,103},{8,40},{... | collective-permute-start | bytes 1376264 | tf_op jit(solution)/shard_map/ppermute | solution.py:138

commit v3 on v2

--- a/solution.py
+++ b/solution.py
@@ -19,14 +19,23 @@
     return ((z * RING + x) * RING + y) * 2 + c
 
 
+def apart(u, v):
+    return sum(min((p - q) % RING, (q - p) % RING) for p, q in zip(u, v))
+
+
 def class_groups():
     groups = []
     for a, b, c in itertools.product(range(2), repeat=3):
-        members = []
+        left = []
         for z, x, y in itertools.product(range(RING), repeat=3):
             if (x + z) % 2 == a and (y + z) % 2 == b:
-                members.append(index(z, x, y, c))
-        groups.append(members)
+                left.append((z, x, y))
+        first, second = [], []
+        while left:
+            chip = left.pop(0)
+            first.append(chip)
+            second.append(left.pop(max(range(len(left)), key=lambda i: apart(left[i], chip))))
+        groups.append([index(z, x, y, c) for z, x, y in first + second])
     return groups
 
 
@@ -64,6 +73,10 @@
     for i in range(out_ref.shape[0]):
         out_ref[i, :, :width] = token
         out_ref[i, :, width:] = scores
+
+
+def sum_kernel(got_ref, out_ref):
+    out_ref[...] = jnp.sum(got_ref[...].astype(jnp.float32), axis=0).astype(jnp.bfloat16)
 
 
 def load_kernel(wg_hbm, wu_hbm, wd_hbm, after_ref, wg, wu, wd, sems):
@@ -187,7 +200,18 @@
         acc = acc + moved(total[a].astype(bf16), neighbour_pairs(a)).astype(f32)
     pieces = acc.astype(bf16).reshape(n, tokens.shape[0], width)
     got = lax.all_to_all(pieces, ALL, split_axis=0, concat_axis=0, axis_index_groups=groups, tiled=True)
-    return jnp.sum(got.astype(f32), axis=0).astype(bf16)
+    lanes = width // LANES
+    pairs = tokens.shape[0] * lanes
+    got = got.reshape(n, tokens.shape[0], lanes, LANES).transpose(0, 2, 1, 3).reshape(n, pairs, LANES)
+    out = pl.pallas_call(
+        sum_kernel,
+        out_shape=jax.ShapeDtypeStruct((pairs, LANES), bf16),
+        in_specs=[VMEM],
+        out_specs=VMEM,
+        compiler_params=LIMIT,
+        name="sum",
+    )(got)
+    return out.reshape(lanes, tokens.shape[0], LANES).transpose(1, 0, 2).reshape(tokens.shape)
 
 
 def solution(mesh):

time: 74.3 us -> 72.1 us (0.970)
  blocking collectives: 40.6 us -> 38.7 us
  other arithmetic: 1.54 us -> 0.54 us
  starting transfers between devices: 6.08 us -> 7.01 us
  waiting for transfers between devices: 16.6 us -> 15.7 us
    all_to_all x1, blocking collectives: 23.2 us -> 21.9 us  [step(): lax.all_to_all(tiled, ALL, split_axis=0, concat_axis=0, axis_index_groups...]
    reduce_sum x1 -> x0, other arithmetic: 1 us -> none  [step(): return jnp.sum(got.astype(f32), axis=0).astype(bf16)]
    ppermute x14, starting transfers between devices: 6.08 us -> 7.01 us  [moved(): return lax.ppermute(block, ALL, pairs)]
    ppermute x14, waiting for transfers between devices: 16.6 us -> 15.7 us  [moved(): return lax.ppermute(block, ALL, pairs)]
  transfers between devices with their start and end apart: 14 -> 14, of which waited for: 6 -> 6; matrix products, arithmetic and copies ran while one was open for 0% -> 0% of each run, Pallas kernels for 10% -> 11%
where the time goes in v3:
time: 72.1 us; the launch traced here: 71.8 us
  blocking collectives  38.7 us (54%)
  waiting for transfers between devices  15.7 us (22%)
  Pallas kernels  9.34 us (13%)
  starting transfers between devices  7.01 us (10%)
    all_to_all x1, blocking collectives, step(): lax.all_to_all(tiled, ALL, split_axis=0, concat_axis=0, axis_index_groups...  21.9 us
    all_to_all x1, blocking collectives, step(): lax.all_to_all(pieces, ALL, split_axis=0, concat_axis=0, axis_index_group...  16.9 us
    ppermute x14, waiting for transfers between devices, moved(): return lax.ppermute(block, ALL, pairs)  15.7 us
    ppermute x14, starting transfers between devices, moved(): return lax.ppermute(block, ALL, pairs)  7.01 us
    pallas_call x1, Pallas kernels, step(): pl.pallas_call(load_kernel, out_shape=[jax.ShapeDtypeStruct(w.shape[1:],...  4.23 us
    pallas_call x2, Pallas kernels, run_experts(): pl.pallas_call(experts_kernel, out_shape=[jax.ShapeDtypeStruct((size, wid...  3.54 us
  transfers between devices with their start and end apart: 14, of which 6 were waited for; matrix products, arithmetic and copies ran while one was open for 0% of the time, Pallas kernels for 11%

profile of v3, /device:TPU:0, one launch (start us, length us, event | category | flops | bytes accessed | tf_op | source)
XLA Modules:
  0.0 71.8 jit_solution(9516403331996000017)
XLA Ops:
  0.0 0.9 %head.1 = bf16[16,2,7296]{2,1,0:T(2,128)(2,1)S(1)} custom-call(s32[1]{0:T(128)} %bitcast.me_ref.refs_7_, bf16[2,7168]{1,0:T(2,128)(2,1)} %tok_hbm.1, s32[2,8]{1,0:T(2,128)} %ids_hbm.1, s32[2,8]{1,0:T(2,128)} %ints_hbm.1), custom_call_target="tpu_custom_call" | custom-call | tf_op jit(solution)/shard_map/head/pallas_call | solution.py:161
  0.9 21.9 %all_to_all.10 = bf16[16,2,7296]{2,1,0:T(2,128)(2,1)S(1)} all-to-all(bf16[16,2,7296]{2,1,0:T(2,128)(2,1)S(1)} %head.1), channel_id=1, replica_groups={{0,4,16,20,42,46,58,62,84,80,68,64,126,122,110,106},{1,5,17,21,43,47,59..., dimensions={0} | all-to-all | bytes 933888 | tf_op jit(solution)/shard_map/all_to_all | solution.py:175
  22.8 0.2 reshape.22.after_ref.refs_1_
  23.0 1.0 %collective-permute-start = (bf16[32,7296]{1,0:T(8,128)(2,1)S(1)}, bf16[32,7296]{1,0:T(8,128)(2,1)S(1)}, u32[]{:S(2)}, u32[]{:S(2)}) collective-permute-start(bf16[32,7296]{1,0:T(8,128)(2,1)S(1)} %reshape.22.after_ref.refs_1_), channel_id=1, source_target_pairs={{0,8},{1,25},{2,10},{3,27},{4,12},{5,29},{6,14},{7,31},{8,0},{9,17... | collective-permute-start | bytes 1400840 | tf_op jit(solution)/shard_map/ppermute | solution.py:151
  24.0 0.2 collective-permute-start.6
  24.2 0.7 collective-permute-start.7
  24.9 0.7 collective-permute-start.2
  25.5 6.1 %collective-permute-done.refs_0_ = bf16[32,7296]{1,0:T(8,128)(2,1)S(1)} collective-permute-done((bf16[32,7296]{1,0:T(8,128)(2,1)S(1)}, bf16[32,7296]{1,0:T(8,128)(2,1)S(1)}, u32[]{:S(2)}, u32[]{:S(2)}) %collective-permute-start) | collective-permute-done | bytes 466976 | tf_op jit(solution)/shard_map/ppermute | solution.py:151
  31.6 0.0 collective-permute-start.1
  31.6 0.9 %collective-permute-done.6.refs_0_ = bf16[32,7296]{1,0:T(8,128)(2,1)S(1)} collective-permute-done((bf16[32,7296]{1,0:T(8,128)(2,1)S(1)}, bf16[32,7296]{1,0:T(8,128)(2,1)S(1)}, u32[]{:S(2)}, u32[]{:S(2)}) %collective-permute-start.6) | collective-permute-done | bytes 466976 | tf_op jit(solution)/shard_map/ppermute | solution.py:151
  32.6 0.2 collective-permute-done.7.refs_1_
  32.7 0.3 collective-permute-start.9
  33.1 4.2 %load.1 = (bf16[7168,256]{1,0:T(8,128)(2,1)S(1)}, bf16[7168,256]{1,0:T(8,128)(2,1)S(1)}, bf16[256,7168]{1,0:T(8,128)(2,1)S(1)}) custom-call(bf16[7168,256]{1,0:T(8,128)(2,1)} %bitcast.15, bf16[7168,256]{1,0:T(8,128)(2,1)} %bitcast.16, bf16[256,7168]{1,0:T(8,128)(2,1)} %bitcast.17, bf16[32,7296]{1,0:T(8,128)(2,1)S(1)} %reshape.22.after_ref.refs_1_), custom_call_target="tpu_custom_call" | custom-call | flops 850000000 | tf_op jit(solution)/shard_map/load/pallas_call | solution.py:177
  37.3 1.8 %shard_map.64 = (f32[32,7168]{1,0:T(8,128)S(1)}, f32[32,7168]{1,0:T(8,128)S(1)}, bf16[32,7168]{1,0:T(8,128)(2,1)S(1)}, bf16[32,7168]{1,0:T(8,128)(2,1)S(1)}) custom-call(s32[1]{0:T(128)} %bitcast.me_ref.refs_7_, bf16[32,7296]{1,0:T(8,128)(2,1)S(1)} %collective-permute-done.refs_0_, bf16[32,7296]{1,0:T(8,128)(2,1)S(1)} %reshape.22.after_ref.refs_1_, ...), custom_call_target="tpu_custom_call" | custom-call | flops 450000000 | tf_op jit(solution)/shard_map/pallas_call | solution.py:124
  39.1 0.3 collective-permute-start.4
  39.4 1.8 %shard_map.65 = (f32[32,7168]{1,0:T(8,128)S(1)}, f32[32,7168]{1,0:T(8,128)S(1)}, bf16[32,7168]{1,0:T(8,128)(2,1)S(1)}, bf16[32,7168]{1,0:T(8,128)(2,1)S(1)}) custom-call(s32[1]{0:T(128)} %bitcast.me_ref.refs_7_, bf16[32,7296]{1,0:T(8,128)(2,1)S(1)} %collective-permute-done.6.refs_0_, bf16[32,7296]{1,0:T(8,128)(2,1)S(1)} %collective-permute-done.7.refs_1_, ...), custom_call_target="tpu_custom_call" | custom-call | flops 450000000 | tf_op jit(solution)/shard_map/pallas_call | solution.py:124
  41.2 0.4 collective-permute-start.10
  41.6 0.2 collective-permute-start.12
  41.8 0.3 collective-permute-start.3
  42.1 0.1 add_convert_fusion.3
  42.2 1.3 %collective-permute-start.5 = (bf16[32,7168]{1,0:T(8,128)(2,1)S(1)}, bf16[32,7168]{1,0:T(8,128)(2,1)S(1)}, u32[]{:S(2)}, u32[]{:S(2)}) collective-permute-start(bf16[32,7168]{1,0:T(8,128)(2,1)S(1)} %add_convert_fusion.3), channel_id=1, source_target_pairs={{0,8},{1,25},{2,10},{3,27},{4,12},{5,29},{6,14},{7,31},{8,0},{9,17... | collective-permute-start | bytes 1376264 | tf_op jit(solution)/shard_map/ppermute | solution.py:151
  43.5 0.1 add_convert_fusion.2
  43.6 1.6 %collective-permute-start.11 = (bf16[32,7168]{1,0:T(8,128)(2,1)S(1)}, bf16[32,7168]{1,0:T(8,128)(2,1)S(1)}, u32[]{:S(2)}, u32[]{:S(2)}) collective-permute-start(bf16[32,7168]{1,0:T(8,128)(2,1)S(1)} %add_convert_fusion.2), channel_id=1, source_target_pairs={{0,2},{1,7},{2,0},{3,5},{4,6},{5,3},{6,4},{7,1},{8,10},{9,15},{10,... | collective-permute-start | bytes 1376264 | tf_op jit(solution)/shard_map/ppermute | solution.py:151
  45.1 0.1 add_convert_fusion.1
  45.2 0.1 collective-permute-start.13
  45.3 5.4 %collective-permute-done.5 = bf16[32,7168]{1,0:T(8,128)(2,1)S(1)} collective-permute-done((bf16[32,7168]{1,0:T(8,128)(2,1)S(1)}, bf16[32,7168]{1,0:T(8,128)(2,1)S(1)}, u32[]{:S(2)}, u32[]{:S(2)}) %collective-permute-start.5) | collective-permute-done | bytes 458784 | tf_op jit(solution)/shard_map/ppermute | solution.py:151
  50.8 1.4 %collective-permute-done.11 = bf16[32,7168]{1,0:T(8,128)(2,1)S(1)} collective-permute-done((bf16[32,7168]{1,0:T(8,128)(2,1)S(1)}, bf16[32,7168]{1,0:T(8,128)(2,1)S(1)}, u32[]{:S(2)}, u32[]{:S(2)}) %collective-permute-start.11) | collective-permute-done | bytes 458784 | tf_op jit(solution)/shard_map/ppermute | solution.py:151
  52.1 1.7 %collective-permute-done.13 = bf16[32,7168]{1,0:T(8,128)(2,1)S(1)} collective-permute-done((bf16[32,7168]{1,0:T(8,128)(2,1)S(1)}, bf16[32,7168]{1,0:T(8,128)(2,1)S(1)}, u32[]{:S(2)}, u32[]{:S(2)}) %collective-permute-start.13) | collective-permute-done | bytes 458784 | tf_op jit(solution)/shard_map/ppermute | solution.py:151
  53.8 0.3 add_convert_fusion
  54.1 0.2 reshape.23
  54.3 16.9 %all_to_all.11 = bf16[16,2,7168]{2,1,0:T(2,128)(2,1)S(1)} all-to-all(bf16[16,2,7168]{2,1,0:T(2,128)(2,1)S(1)} %reshape.23), channel_id=1, replica_groups={{0,4,16,20,42,46,58,62,84,80,68,64,126,122,110,106},{1,5,17,21,43,47,59..., dimensions={0} | all-to-all | bytes 917504 | tf_op jit(solution)/shard_map/all_to_all | solution.py:202
  71.1 0.7 sum.1
  (9 shorter events, 0.0 us)
Async XLA Ops:
  23.0 8.6 %collective-permute-start = (bf16[32,7296]{1,0:T(8,128)(2,1)S(1)}, bf16[32,7296]{1,0:T(8,128)(2,1)S(1)}, u32[]{:S(2)}, u32[]{:S(2)}) collective-permute-start(bf16[32,7296]{1,0:T(8,128)(2,1)S(1)} %reshape.22.after_ref.refs_1_), channel_id=1, source_target_pairs={{0,8},{1,25},{2,10},{3,27},{4,12},{5,29},{6,14},{7,31},{8,0},{9,17... | collective-permute-start | bytes 1400840 | tf_op jit(solution)/shard_map/ppermute | solution.py:151
  24.0 8.6 %collective-permute-start.6 = (bf16[32,7296]{1,0:T(8,128)(2,1)S(1)}, bf16[32,7296]{1,0:T(8,128)(2,1)S(1)}, u32[]{:S(2)}, u32[]{:S(2)}) collective-permute-start(bf16[32,7296]{1,0:T(8,128)(2,1)S(1)} %reshape.22.after_ref.refs_1_), channel_id=1, source_target_pairs={{0,2},{1,7},{2,0},{3,5},{4,6},{5,3},{6,4},{7,1},{8,10},{9,15},{10,... | collective-permute-start | bytes 1400840 | tf_op jit(solution)/shard_map/ppermute | solution.py:151
  24.2 8.6 %collective-permute-start.7 = (bf16[32,7296]{1,0:T(8,128)(2,1)S(1)}, bf16[32,7296]{1,0:T(8,128)(2,1)S(1)}, u32[]{:S(2)}, u32[]{:S(2)}) collective-permute-start(bf16[32,7296]{1,0:T(8,128)(2,1)S(1)} %reshape.22.after_ref.refs_1_), channel_id=1, source_target_pairs={{0,32},{1,97},{2,34},{3,99},{4,36},{5,101},{6,38},{7,103},{8,40},{... | collective-permute-start | bytes 1400840 | tf_op jit(solution)/shard_map/ppermute | solution.py:151
  24.9 12.4 %collective-permute-start.2 = (bf16[32,7296]{1,0:T(8,128)(2,1)S(1)}, bf16[32,7296]{1,0:T(8,128)(2,1)S(1)}, u32[]{:S(2)}, u32[]{:S(2)}) collective-permute-start(bf16[32,7296]{1,0:T(8,128)(2,1)S(1)} %reshape.22.after_ref.refs_1_), channel_id=1, source_target_pairs={{0,1},{1,0},{2,3},{3,2},{4,5},{5,4},{6,7},{7,6},{8,9},{9,8},{10,11... | collective-permute-start | bytes 1400840 | tf_op jit(solution)/shard_map/ppermute | solution.py:151
  31.6 5.7 %collective-permute-start.1 = (bf16[32,7296]{1,0:T(8,128)(2,1)S(1)}, bf16[32,7296]{1,0:T(8,128)(2,1)S(1)}, u32[]{:S(2)}, u32[]{:S(2)}) collective-permute-start(bf16[32,7296]{1,0:T(8,128)(2,1)S(1)} %collective-permute-done.refs_0_), channel_id=1, source_target_pairs={{0,1},{1,0},{2,3},{3,2},{4,5},{5,4},{6,7},{7,6},{8,9},{9,8},{10,11... | collective-permute-start | bytes 1400840 | tf_op jit(solution)/shard_map/ppermute | solution.py:151
  32.6 6.8 %collective-permute-start.8 = (bf16[32,7296]{1,0:T(8,128)(2,1)S(1)}, bf16[32,7296]{1,0:T(8,128)(2,1)S(1)}, u32[]{:S(2)}, u32[]{:S(2)}) collective-permute-start(bf16[32,7296]{1,0:T(8,128)(2,1)S(1)} %collective-permute-done.6.refs_0_), channel_id=1, source_target_pairs={{0,1},{1,0},{2,3},{3,2},{4,5},{5,4},{6,7},{7,6},{8,9},{9,8},{10,11... | collective-permute-start | bytes 1400840 | tf_op jit(solution)/shard_map/ppermute | solution.py:151
  32.7 6.6 %collective-permute-start.9 = (bf16[32,7296]{1,0:T(8,128)(2,1)S(1)}, bf16[32,7296]{1,0:T(8,128)(2,1)S(1)}, u32[]{:S(2)}, u32[]{:S(2)}) collective-permute-start(bf16[32,7296]{1,0:T(8,128)(2,1)S(1)} %collective-permute-done.7.refs_1_), channel_id=1, source_target_pairs={{0,1},{1,0},{2,3},{3,2},{4,5},{5,4},{6,7},{7,6},{8,9},{9,8},{10,11... | collective-permute-start | bytes 1400840 | tf_op jit(solution)/shard_map/ppermute | solution.py:151
  39.1 3.0 %collective-permute-start.4 = (bf16[32,7168]{1,0:T(8,128)(2,1)S(1)}, bf16[32,7168]{1,0:T(8,128)(2,1)S(1)}, u32[]{:S(2)}, u32[]{:S(2)}) collective-permute-start(bf16[32,7168]{1,0:T(8,128)(2,1)S(1)} %get-tuple-element.22.refs_7_), channel_id=1, source_target_pairs={{0,1},{1,0},{2,3},{3,2},{4,5},{5,4},{6,7},{7,6},{8,9},{9,8},{10,11... | collective-permute-start | bytes 1376264 | tf_op jit(solution)/shard_map/ppermute | solution.py:151
  41.2 2.3 %collective-permute-start.10 = (bf16[32,7168]{1,0:T(8,128)(2,1)S(1)}, bf16[32,7168]{1,0:T(8,128)(2,1)S(1)}, u32[]{:S(2)}, u32[]{:S(2)}) collective-permute-start(bf16[32,7168]{1,0:T(8,128)(2,1)S(1)} %get-tuple-element.24), channel_id=1, source_target_pairs={{0,1},{1,0},{2,3},{3,2},{4,5},{5,4},{6,7},{7,6},{8,9},{9,8},{10,11... | collective-permute-start | bytes 1376264 | tf_op jit(solution)/shard_map/ppermute | solution.py:151
  41.6 3.6 %collective-permute-start.12 = (bf16[32,7168]{1,0:T(8,128)(2,1)S(1)}, bf16[32,7168]{1,0:T(8,128)(2,1)S(1)}, u32[]{:S(2)}, u32[]{:S(2)}) collective-permute-start(bf16[32,7168]{1,0:T(8,128)(2,1)S(1)} %get-tuple-element.26), channel_id=1, source_target_pairs={{0,1},{1,0},{2,3},{3,2},{4,5},{5,4},{6,7},{7,6},{8,9},{9,8},{10,11... | collective-permute-start | bytes 1376264 | tf_op jit(solution)/shard_map/ppermute | solution.py:151
  41.8 3.6 %collective-permute-start.3 = (bf16[32,7168]{1,0:T(8,128)(2,1)S(1)}, bf16[32,7168]{1,0:T(8,128)(2,1)S(1)}, u32[]{:S(2)}, u32[]{:S(2)}) collective-permute-start(bf16[32,7168]{1,0:T(8,128)(2,1)S(1)} %get-tuple-element.20), channel_id=1, source_target_pairs={{0,1},{1,0},{2,3},{3,2},{4,5},{5,4},{6,7},{7,6},{8,9},{9,8},{10,11... | collective-permute-start | bytes 1376264 | tf_op jit(solution)/shard_map/ppermute | solution.py:151
  42.2 8.6 %collective-permute-start.5 = (bf16[32,7168]{1,0:T(8,128)(2,1)S(1)}, bf16[32,7168]{1,0:T(8,128)(2,1)S(1)}, u32[]{:S(2)}, u32[]{:S(2)}) collective-permute-start(bf16[32,7168]{1,0:T(8,128)(2,1)S(1)} %add_convert_fusion.3), channel_id=1, source_target_pairs={{0,8},{1,25},{2,10},{3,27},{4,12},{5,29},{6,14},{7,31},{8,0},{9,17... | collective-permute-start | bytes 1376264 | tf_op jit(solution)/shard_map/ppermute | solution.py:151
  43.6 8.6 %collective-permute-start.11 = (bf16[32,7168]{1,0:T(8,128)(2,1)S(1)}, bf16[32,7168]{1,0:T(8,128)(2,1)S(1)}, u32[]{:S(2)}, u32[]{:S(2)}) collective-permute-start(bf16[32,7168]{1,0:T(8,128)(2,1)S(1)} %add_convert_fusion.2), channel_id=1, source_target_pairs={{0,2},{1,7},{2,0},{3,5},{4,6},{5,3},{6,4},{7,1},{8,10},{9,15},{10,... | collective-permute-start | bytes 1376264 | tf_op jit(solution)/shard_map/ppermute | solution.py:151
  45.2 8.6 %collective-permute-start.13 = (bf16[32,7168]{1,0:T(8,128)(2,1)S(1)}, bf16[32,7168]{1,0:T(8,128)(2,1)S(1)}, u32[]{:S(2)}, u32[]{:S(2)}) collective-permute-start(bf16[32,7168]{1,0:T(8,128)(2,1)S(1)} %add_convert_fusion.1), channel_id=1, source_target_pairs={{0,32},{1,97},{2,34},{3,99},{4,36},{5,101},{6,38},{7,103},{8,40},{... | collective-permute-start | bytes 1376264 | tf_op jit(solution)/shard_map/ppermute | solution.py:151

commit v4 on v3

--- a/solution.py
+++ b/solution.py
@@ -12,6 +12,7 @@
 RING = 4
 LANES = 128
 KCH = 1024
+DOWN = 3584
 RATE = 250
 
 
@@ -79,6 +80,18 @@
     out_ref[...] = jnp.sum(got_ref[...].astype(jnp.float32), axis=0).astype(jnp.bfloat16)
 
 
+def add_kernel(kept, b0, b1, b2, b3, out_ref):
+    rows = out_ref.shape[1]
+    for i in range(kept.shape[1] // KCH):
+        ks = pl.ds(i * KCH, KCH)
+        acc = kept[:, ks]
+        for ref in (b0, b1, b2, b3):
+            acc = acc + ref[:, ks].astype(jnp.float32)
+        acc = acc.astype(jnp.bfloat16)
+        for j in range(out_ref.shape[0]):
+            out_ref[j, :, ks] = acc[j * rows:(j + 1) * rows]
+
+
 def load_kernel(wg_hbm, wu_hbm, wd_hbm, after_ref, wg, wu, wd, sems):
     copies = [
         pltpu.make_async_copy(src, dst, sems.at[i])
@@ -110,8 +123,8 @@
         u = jnp.dot(part, wu[ks, :], preferred_element_type=jnp.float32)
         gate, up = (g, u) if gate is None else (gate + g, up + u)
     hid[...] = (gate / (1.0 + jnp.exp(-gate)) * up).astype(jnp.bfloat16)
-    for i in range(width // KCH):
-        ks = pl.ds(i * KCH, KCH)
+    for i in range(width // DOWN):
+        ks = pl.ds(i * DOWN, DOWN)
         out = jnp.dot(hid[...], wd[:, ks], preferred_element_type=jnp.float32) * weight
         for j, ref in enumerate(outs):
             ref[:, ks] = out[j * size:(j + 1) * size].astype(ref.dtype)
@@ -185,20 +198,26 @@
         name="load",
     )(*in_hbm(w_gate[0], w_up[0], w_down[0]), own)
 
-    near = {a: moved(own, neighbour_pairs(a)) for a in "xyz"}
+    near = {a: moved(own, neighbour_pairs(a)) for a in "yzx"}
     near["o"] = own
     swapped = {a: moved(b, swap_pairs()) for a, b in near.items()}
-    total = {}
+    total, parts = {}, {}
     after = me
-    for pair in ("xo", "yz"):
+    for pair in ("yo", "zx"):
         mine, theirs = run_experts(me, [near[a] for a in pair], [swapped[a] for a in pair], (wg, wu, wd), after)
         after = theirs[0]
         for a, kept, sent in zip(pair, mine, theirs):
-            total[a] = kept + moved(sent, swap_pairs()).astype(f32)
-    acc = total["o"]
-    for a in "xyz":
-        acc = acc + moved(total[a].astype(bf16), neighbour_pairs(a)).astype(f32)
-    pieces = acc.astype(bf16).reshape(n, tokens.shape[0], width)
+            parts[a] = (kept, moved(sent, swap_pairs()))
+            total[a] = parts[a][0] + parts[a][1].astype(f32)
+    arrived = [moved(total[a].astype(bf16), neighbour_pairs(a)) for a in "yzx"]
+    pieces = pl.pallas_call(
+        add_kernel,
+        out_shape=jax.ShapeDtypeStruct((n, tokens.shape[0], width), bf16),
+        in_specs=[VMEM] * 5,
+        out_specs=VMEM,
+        compiler_params=LIMIT,
+        name="add",
+    )(*parts["o"], *arrived)
     got = lax.all_to_all(pieces, ALL, split_axis=0, concat_axis=0, axis_index_groups=groups, tiled=True)
     lanes = width // LANES
     pairs = tokens.shape[0] * lanes

time: 72.1 us -> 71.8 us (level)
  starting transfers between devices: 7.01 us -> 8.41 us
  waiting for transfers between devices: 15.7 us -> 14.3 us
    ppermute x14, starting transfers between devices: 7.01 us -> 8.41 us  [moved(): return lax.ppermute(block, ALL, pairs)]
    ppermute x14, waiting for transfers between devices: 15.7 us -> 14.3 us  [moved(): return lax.ppermute(block, ALL, pairs)]
where the time goes in v4:
time: 71.8 us; the launch traced here: 71.6 us
  blocking collectives  38.7 us (54%)
  waiting for transfers between devices  14.3 us (20%)
  Pallas kernels  9.66 us (13%)
  starting transfers between devices  8.41 us (12%)
    all_to_all x1, blocking collectives, step(): lax.all_to_all(tiled, ALL, split_axis=0, concat_axis=0, axis_index_groups...  21.9 us
    all_to_all x1, blocking collectives, step(): lax.all_to_all(pieces, ALL, split_axis=0, concat_axis=0, axis_index_group...  16.8 us
    ppermute x14, waiting for transfers between devices, moved(): return lax.ppermute(block, ALL, pairs)  14.3 us
    ppermute x14, starting transfers between devices, moved(): return lax.ppermute(block, ALL, pairs)  8.41 us
    pallas_call x1, Pallas kernels, step(): pl.pallas_call(load_kernel, out_shape=[jax.ShapeDtypeStruct(w.shape[1:],...  4.23 us
    pallas_call x2, Pallas kernels, run_experts(): pl.pallas_call(experts_kernel, out_shape=[jax.ShapeDtypeStruct((size, wid...  3.54 us
  transfers between devices with their start and end apart: 14, of which 6 were waited for; matrix products, arithmetic and copies ran while one was open for 0% of the time, Pallas kernels for 11%

profile of v4, /device:TPU:0, one launch (start us, length us, event | category | flops | bytes accessed | tf_op | source)
XLA Modules:
  0.0 71.6 jit_solution(1951256014390878586)
XLA Ops:
  0.0 0.9 %head.1 = bf16[16,2,7296]{2,1,0:T(2,128)(2,1)S(1)} custom-call(s32[1]{0:T(128)} %bitcast.me_ref.refs_7_, bf16[2,7168]{1,0:T(2,128)(2,1)} %tok_hbm.1, s32[2,8]{1,0:T(2,128)} %ids_hbm.1, s32[2,8]{1,0:T(2,128)} %ints_hbm.1), custom_call_target="tpu_custom_call" | custom-call | tf_op jit(solution)/shard_map/head/pallas_call | solution.py:174
  0.9 21.9 %all_to_all.10 = bf16[16,2,7296]{2,1,0:T(2,128)(2,1)S(1)} all-to-all(bf16[16,2,7296]{2,1,0:T(2,128)(2,1)S(1)} %head.1), channel_id=1, replica_groups={{0,4,16,20,42,46,58,62,84,80,68,64,126,122,110,106},{1,5,17,21,43,47,59..., dimensions={0} | all-to-all | bytes 933888 | tf_op jit(solution)/shard_map/all_to_all | solution.py:188
  22.8 0.2 reshape.19.after_ref.refs_1_
  23.0 0.6 collective-permute-start
  23.6 0.1 collective-permute-start.6
  23.7 1.2 %collective-permute-start.7 = (bf16[32,7296]{1,0:T(8,128)(2,1)S(1)}, bf16[32,7296]{1,0:T(8,128)(2,1)S(1)}, u32[]{:S(2)}, u32[]{:S(2)}) collective-permute-start(bf16[32,7296]{1,0:T(8,128)(2,1)S(1)} %reshape.19.after_ref.refs_1_), channel_id=1, source_target_pairs={{0,8},{1,25},{2,10},{3,27},{4,12},{5,29},{6,14},{7,31},{8,0},{9,17... | collective-permute-start | bytes 1400840 | tf_op jit(solution)/shard_map/ppermute | solution.py:164
  24.9 0.7 collective-permute-start.2
  25.5 6.1 %collective-permute-done.refs_0_ = bf16[32,7296]{1,0:T(8,128)(2,1)S(1)} collective-permute-done((bf16[32,7296]{1,0:T(8,128)(2,1)S(1)}, bf16[32,7296]{1,0:T(8,128)(2,1)S(1)}, u32[]{:S(2)}, u32[]{:S(2)}) %collective-permute-start) | collective-permute-done | bytes 466976 | tf_op jit(solution)/shard_map/ppermute | solution.py:164
  31.6 0.0 collective-permute-start.1
  31.6 0.5 collective-permute-done.6.refs_0_
  32.2 0.1 collective-permute-done.7.refs_1_
  32.3 0.4 collective-permute-start.9
  32.7 4.2 %load.1 = (bf16[7168,256]{1,0:T(8,128)(2,1)S(1)}, bf16[7168,256]{1,0:T(8,128)(2,1)S(1)}, bf16[256,7168]{1,0:T(8,128)(2,1)S(1)}) custom-call(bf16[7168,256]{1,0:T(8,128)(2,1)} %bitcast.15, bf16[7168,256]{1,0:T(8,128)(2,1)} %bitcast.16, bf16[256,7168]{1,0:T(8,128)(2,1)} %bitcast.17, bf16[32,7296]{1,0:T(8,128)(2,1)S(1)} %reshape.19.after_ref.refs_1_), custom_call_target="tpu_custom_call" | custom-call | flops 850000000 | tf_op jit(solution)/shard_map/load/pallas_call | solution.py:190
  36.9 0.0 collective-permute-done.1.refs_2_
  36.9 1.8 %shard_map.64 = (f32[32,7168]{1,0:T(8,128)S(1)}, f32[32,7168]{1,0:T(8,128)S(1)}, bf16[32,7168]{1,0:T(8,128)(2,1)S(1)}, bf16[32,7168]{1,0:T(8,128)(2,1)S(1)}) custom-call(s32[1]{0:T(128)} %bitcast.me_ref.refs_7_, bf16[32,7296]{1,0:T(8,128)(2,1)S(1)} %collective-permute-done.refs_0_, bf16[32,7296]{1,0:T(8,128)(2,1)S(1)} %reshape.19.after_ref.refs_1_, ...), custom_call_target="tpu_custom_call" | custom-call | flops 450000000 | tf_op jit(solution)/shard_map/pallas_call | solution.py:137
  38.7 0.2 collective-permute-start.4
  38.9 0.4 collective-permute-start.3
  39.3 1.8 %shard_map.65 = (f32[32,7168]{1,0:T(8,128)S(1)}, f32[32,7168]{1,0:T(8,128)S(1)}, bf16[32,7168]{1,0:T(8,128)(2,1)S(1)}, bf16[32,7168]{1,0:T(8,128)(2,1)S(1)}) custom-call(s32[1]{0:T(128)} %bitcast.me_ref.refs_7_, bf16[32,7296]{1,0:T(8,128)(2,1)S(1)} %collective-permute-done.6.refs_0_, bf16[32,7296]{1,0:T(8,128)(2,1)S(1)} %collective-permute-done.7.refs_1_, ...), custom_call_target="tpu_custom_call" | custom-call | flops 450000000 | tf_op jit(solution)/shard_map/pallas_call | solution.py:137
  41.1 0.2 collective-permute-start.10
  41.3 0.4 collective-permute-start.12
  41.7 0.1 add_convert_fusion.2
  41.8 1.6 %collective-permute-start.5 = (bf16[32,7168]{1,0:T(8,128)(2,1)S(1)}, bf16[32,7168]{1,0:T(8,128)(2,1)S(1)}, u32[]{:S(2)}, u32[]{:S(2)}) collective-permute-start(bf16[32,7168]{1,0:T(8,128)(2,1)S(1)} %add_convert_fusion.2), channel_id=1, source_target_pairs={{0,2},{1,7},{2,0},{3,5},{4,6},{5,3},{6,4},{7,1},{8,10},{9,15},{10,... | collective-permute-start | bytes 1376264 | tf_op jit(solution)/shard_map/ppermute | solution.py:164
  43.4 0.1 add_convert_fusion.1
  43.5 1.7 %collective-permute-start.11 = (bf16[32,7168]{1,0:T(8,128)(2,1)S(1)}, bf16[32,7168]{1,0:T(8,128)(2,1)S(1)}, u32[]{:S(2)}, u32[]{:S(2)}) collective-permute-start(bf16[32,7168]{1,0:T(8,128)(2,1)S(1)} %add_convert_fusion.1), channel_id=1, source_target_pairs={{0,32},{1,97},{2,34},{3,99},{4,36},{5,101},{6,38},{7,103},{8,40},{... | collective-permute-start | bytes 1376264 | tf_op jit(solution)/shard_map/ppermute | solution.py:164
  45.2 0.1 add_convert_fusion
  45.3 1.0 %collective-permute-start.13 = (bf16[32,7168]{1,0:T(8,128)(2,1)S(1)}, bf16[32,7168]{1,0:T(8,128)(2,1)S(1)}, u32[]{:S(2)}, u32[]{:S(2)}) collective-permute-start(bf16[32,7168]{1,0:T(8,128)(2,1)S(1)} %add_convert_fusion), channel_id=1, source_target_pairs={{0,8},{1,25},{2,10},{3,27},{4,12},{5,29},{6,14},{7,31},{8,0},{9,17... | collective-permute-start | bytes 1376264 | tf_op jit(solution)/shard_map/ppermute | solution.py:164
  46.3 4.0 %collective-permute-done.5.b1 = bf16[32,7168]{1,0:T(8,128)(2,1)S(1)} collective-permute-done((bf16[32,7168]{1,0:T(8,128)(2,1)S(1)}, bf16[32,7168]{1,0:T(8,128)(2,1)S(1)}, u32[]{:S(2)}, u32[]{:S(2)}) %collective-permute-start.5) | collective-permute-done | bytes 458784 | tf_op jit(solution)/shard_map/ppermute | solution.py:164
  50.3 1.7 %collective-permute-done.11.b2 = bf16[32,7168]{1,0:T(8,128)(2,1)S(1)} collective-permute-done((bf16[32,7168]{1,0:T(8,128)(2,1)S(1)}, bf16[32,7168]{1,0:T(8,128)(2,1)S(1)}, u32[]{:S(2)}, u32[]{:S(2)}) %collective-permute-start.11) | collective-permute-done | bytes 458784 | tf_op jit(solution)/shard_map/ppermute | solution.py:164
  52.0 1.8 %collective-permute-done.13.b3 = bf16[32,7168]{1,0:T(8,128)(2,1)S(1)} collective-permute-done((bf16[32,7168]{1,0:T(8,128)(2,1)S(1)}, bf16[32,7168]{1,0:T(8,128)(2,1)S(1)}, u32[]{:S(2)}, u32[]{:S(2)}) %collective-permute-start.13) | collective-permute-done | bytes 458784 | tf_op jit(solution)/shard_map/ppermute | solution.py:164
  53.8 0.3 add.20
  54.2 16.8 %all_to_all.11 = bf16[16,2,7168]{2,1,0:T(2,128)(2,1)S(1)} all-to-all(bf16[16,2,7168]{2,1,0:T(2,128)(2,1)S(1)} %add.20), channel_id=1, replica_groups={{0,4,16,20,42,46,58,62,84,80,68,64,126,122,110,106},{1,5,17,21,43,47,59..., dimensions={0} | all-to-all | bytes 917504 | tf_op jit(solution)/shard_map/all_to_all | solution.py:221
  70.9 0.7 sum.1
  (8 shorter events, 0.0 us)
Async XLA Ops:
  23.0 8.6 %collective-permute-start = (bf16[32,7296]{1,0:T(8,128)(2,1)S(1)}, bf16[32,7296]{1,0:T(8,128)(2,1)S(1)}, u32[]{:S(2)}, u32[]{:S(2)}) collective-permute-start(bf16[32,7296]{1,0:T(8,128)(2,1)S(1)} %reshape.19.after_ref.refs_1_), channel_id=1, source_target_pairs={{0,2},{1,7},{2,0},{3,5},{4,6},{5,3},{6,4},{7,1},{8,10},{9,15},{10,... | collective-permute-start | bytes 1400840 | tf_op jit(solution)/shard_map/ppermute | solution.py:164
  23.6 8.6 %collective-permute-start.6 = (bf16[32,7296]{1,0:T(8,128)(2,1)S(1)}, bf16[32,7296]{1,0:T(8,128)(2,1)S(1)}, u32[]{:S(2)}, u32[]{:S(2)}) collective-permute-start(bf16[32,7296]{1,0:T(8,128)(2,1)S(1)} %reshape.19.after_ref.refs_1_), channel_id=1, source_target_pairs={{0,32},{1,97},{2,34},{3,99},{4,36},{5,101},{6,38},{7,103},{8,40},{... | collective-permute-start | bytes 1400840 | tf_op jit(solution)/shard_map/ppermute | solution.py:164
  23.7 8.6 %collective-permute-start.7 = (bf16[32,7296]{1,0:T(8,128)(2,1)S(1)}, bf16[32,7296]{1,0:T(8,128)(2,1)S(1)}, u32[]{:S(2)}, u32[]{:S(2)}) collective-permute-start(bf16[32,7296]{1,0:T(8,128)(2,1)S(1)} %reshape.19.after_ref.refs_1_), channel_id=1, source_target_pairs={{0,8},{1,25},{2,10},{3,27},{4,12},{5,29},{6,14},{7,31},{8,0},{9,17... | collective-permute-start | bytes 1400840 | tf_op jit(solution)/shard_map/ppermute | solution.py:164
  24.9 12.0 %collective-permute-start.2 = (bf16[32,7296]{1,0:T(8,128)(2,1)S(1)}, bf16[32,7296]{1,0:T(8,128)(2,1)S(1)}, u32[]{:S(2)}, u32[]{:S(2)}) collective-permute-start(bf16[32,7296]{1,0:T(8,128)(2,1)S(1)} %reshape.19.after_ref.refs_1_), channel_id=1, source_target_pairs={{0,1},{1,0},{2,3},{3,2},{4,5},{5,4},{6,7},{7,6},{8,9},{9,8},{10,11... | collective-permute-start | bytes 1400840 | tf_op jit(solution)/shard_map/ppermute | solution.py:164
  31.6 5.3 %collective-permute-start.1 = (bf16[32,7296]{1,0:T(8,128)(2,1)S(1)}, bf16[32,7296]{1,0:T(8,128)(2,1)S(1)}, u32[]{:S(2)}, u32[]{:S(2)}) collective-permute-start(bf16[32,7296]{1,0:T(8,128)(2,1)S(1)} %collective-permute-done.refs_0_), channel_id=1, source_target_pairs={{0,1},{1,0},{2,3},{3,2},{4,5},{5,4},{6,7},{7,6},{8,9},{9,8},{10,11... | collective-permute-start | bytes 1400840 | tf_op jit(solution)/shard_map/ppermute | solution.py:164
  32.2 7.1 %collective-permute-start.8 = (bf16[32,7296]{1,0:T(8,128)(2,1)S(1)}, bf16[32,7296]{1,0:T(8,128)(2,1)S(1)}, u32[]{:S(2)}, u32[]{:S(2)}) collective-permute-start(bf16[32,7296]{1,0:T(8,128)(2,1)S(1)} %collective-permute-done.6.refs_0_), channel_id=1, source_target_pairs={{0,1},{1,0},{2,3},{3,2},{4,5},{5,4},{6,7},{7,6},{8,9},{9,8},{10,11... | collective-permute-start | bytes 1400840 | tf_op jit(solution)/shard_map/ppermute | solution.py:164
  32.3 7.0 %collective-permute-start.9 = (bf16[32,7296]{1,0:T(8,128)(2,1)S(1)}, bf16[32,7296]{1,0:T(8,128)(2,1)S(1)}, u32[]{:S(2)}, u32[]{:S(2)}) collective-permute-start(bf16[32,7296]{1,0:T(8,128)(2,1)S(1)} %collective-permute-done.7.refs_1_), channel_id=1, source_target_pairs={{0,1},{1,0},{2,3},{3,2},{4,5},{5,4},{6,7},{7,6},{8,9},{9,8},{10,11... | collective-permute-start | bytes 1400840 | tf_op jit(solution)/shard_map/ppermute | solution.py:164
  38.7 3.0 %collective-permute-start.4 = (bf16[32,7168]{1,0:T(8,128)(2,1)S(1)}, bf16[32,7168]{1,0:T(8,128)(2,1)S(1)}, u32[]{:S(2)}, u32[]{:S(2)}) collective-permute-start(bf16[32,7168]{1,0:T(8,128)(2,1)S(1)} %get-tuple-element.22.refs_7_), channel_id=1, source_target_pairs={{0,1},{1,0},{2,3},{3,2},{4,5},{5,4},{6,7},{7,6},{8,9},{9,8},{10,11... | collective-permute-start | bytes 1376264 | tf_op jit(solution)/shard_map/ppermute | solution.py:164
  38.9 7.4 %collective-permute-start.3 = (bf16[32,7168]{1,0:T(8,128)(2,1)S(1)}, bf16[32,7168]{1,0:T(8,128)(2,1)S(1)}, u32[]{:S(2)}, u32[]{:S(2)}) collective-permute-start(bf16[32,7168]{1,0:T(8,128)(2,1)S(1)} %get-tuple-element.20), channel_id=1, source_target_pairs={{0,1},{1,0},{2,3},{3,2},{4,5},{5,4},{6,7},{7,6},{8,9},{9,8},{10,11... | collective-permute-start | bytes 1376264 | tf_op jit(solution)/shard_map/ppermute | solution.py:164
  41.1 2.3 %collective-permute-start.10 = (bf16[32,7168]{1,0:T(8,128)(2,1)S(1)}, bf16[32,7168]{1,0:T(8,128)(2,1)S(1)}, u32[]{:S(2)}, u32[]{:S(2)}) collective-permute-start(bf16[32,7168]{1,0:T(8,128)(2,1)S(1)} %get-tuple-element.24), channel_id=1, source_target_pairs={{0,1},{1,0},{2,3},{3,2},{4,5},{5,4},{6,7},{7,6},{8,9},{9,8},{10,11... | collective-permute-start | bytes 1376264 | tf_op jit(solution)/shard_map/ppermute | solution.py:164
  41.3 3.9 %collective-permute-start.12 = (bf16[32,7168]{1,0:T(8,128)(2,1)S(1)}, bf16[32,7168]{1,0:T(8,128)(2,1)S(1)}, u32[]{:S(2)}, u32[]{:S(2)}) collective-permute-start(bf16[32,7168]{1,0:T(8,128)(2,1)S(1)} %get-tuple-element.26), channel_id=1, source_target_pairs={{0,1},{1,0},{2,3},{3,2},{4,5},{5,4},{6,7},{7,6},{8,9},{9,8},{10,11... | collective-permute-start | bytes 1376264 | tf_op jit(solution)/shard_map/ppermute | solution.py:164
  41.8 8.6 %collective-permute-start.5 = (bf16[32,7168]{1,0:T(8,128)(2,1)S(1)}, bf16[32,7168]{1,0:T(8,128)(2,1)S(1)}, u32[]{:S(2)}, u32[]{:S(2)}) collective-permute-start(bf16[32,7168]{1,0:T(8,128)(2,1)S(1)} %add_convert_fusion.2), channel_id=1, source_target_pairs={{0,2},{1,7},{2,0},{3,5},{4,6},{5,3},{6,4},{7,1},{8,10},{9,15},{10,... | collective-permute-start | bytes 1376264 | tf_op jit(solution)/shard_map/ppermute | solution.py:164
  43.5 8.6 %collective-permute-start.11 = (bf16[32,7168]{1,0:T(8,128)(2,1)S(1)}, bf16[32,7168]{1,0:T(8,128)(2,1)S(1)}, u32[]{:S(2)}, u32[]{:S(2)}) collective-permute-start(bf16[32,7168]{1,0:T(8,128)(2,1)S(1)} %add_convert_fusion.1), channel_id=1, source_target_pairs={{0,32},{1,97},{2,34},{3,99},{4,36},{5,101},{6,38},{7,103},{8,40},{... | collective-permute-start | bytes 1376264 | tf_op jit(solution)/shard_map/ppermute | solution.py:164
  45.3 8.6 %collective-permute-start.13 = (bf16[32,7168]{1,0:T(8,128)(2,1)S(1)}, bf16[32,7168]{1,0:T(8,128)(2,1)S(1)}, u32[]{:S(2)}, u32[]{:S(2)}) collective-permute-start(bf16[32,7168]{1,0:T(8,128)(2,1)S(1)} %add_convert_fusion), channel_id=1, source_target_pairs={{0,8},{1,25},{2,10},{3,27},{4,12},{5,29},{6,14},{7,31},{8,0},{9,17... | collective-permute-start | bytes 1376264 | tf_op jit(solution)/shard_map/ppermute | solution.py:164
